TPU v7x, 64 devices: a 2x2x8 block of a 4x4x8 slice. The times are simulated.
64 devices in a mesh: dp: 4 (over x, y), ep: 16 (over z, core).
Axes of the slice: x: 2, y: 2, z: 8, core: 2. Of those that a mesh axis runs over, the one named last changes fastest.
The devices are a block of a 4x4x8 slice.
Arguments:
- hidden: bfloat16 [8192, 1024], P(('dp', 'ep')), parts along dimension 0
- k_cache: bfloat16 [8192, 32, 8, 64], P(('dp', 'ep')), parts along dimension 0
- v_cache: bfloat16 [8192, 32, 8, 64], P(('dp', 'ep')), parts along dimension 0
- seq_lens: int32 [8192], P(('dp', 'ep')), parts along dimension 0
- expert_ids: int32 [8192, 8], P(('dp', 'ep')), parts along dimension 0
- ln_attn: bfloat16 [1024], replicated
- w_q: bfloat16 [1024, 1024], replicated
- w_k: bfloat16 [1024, 512], replicated
- w_v: bfloat16 [1024, 512], replicated
- q_gain: bfloat16 [64], replicated
- k_gain: bfloat16 [64], replicated
- w_o: bfloat16 [1024, 1024], replicated
- ln_moe: bfloat16 [1024], replicated
- w_router: bfloat16 [1024, 32], replicated
- w_gate: bfloat16 [32, 1024, 512], P('ep')
- w_up: bfloat16 [32, 1024, 512], P('ep')
- w_down: bfloat16 [32, 512, 1024], P('ep')
Outputs:
- output 1: bfloat16 [8192, 1024], P(('dp', 'ep')), parts along dimension 0
- output 2: bfloat16 [8192, 32, 8, 64], P(('dp', 'ep')), parts along dimension 0
- output 3: bfloat16 [8192, 32, 8, 64], P(('dp', 'ep')), parts along dimension 0
There are 4 independent parts. A program takes and returns all parts, laid end to end along the dimension named above; an argument that names none is the same for every part.
All inputs are finite; a program needn't handle non-finite values.
Results may differ from a plain program's by a relative error of at most 0.00558231.
Values are sent between devices in bfloat16 or wider.
A program may use at most 768 MiB of HBM per device.

v0:
```python
import jax
import jax.numpy as jnp
from jax import lax
from jax.sharding import PartitionSpec as P

EPS = 1e-6
ROPE_BASE = 1000000.0


def rms_scale(values, gain_vec):
    mean_sq = jnp.mean(values * values, axis=-1, keepdims=True)
    return values * lax.rsqrt(mean_sq + EPS) * gain_vec.astype(jnp.float32)


def rotate_half(values, angles):
    half_dim = values.shape[-1] // 2
    x_low = values[..., :half_dim]
    x_high = values[..., half_dim:]
    cos_val = jnp.cos(angles)
    sin_val = jnp.sin(angles)
    return jnp.concatenate([x_low * cos_val - x_high * sin_val, x_high * cos_val + x_low * sin_val], axis=-1)


def attend(hidden, k_cache, v_cache, seq_lens, ln_attn, w_q, w_k, w_v, q_gain, k_gain, w_o):
    n_seq = hidden.shape[0]
    t_max = k_cache.shape[1]
    head_dim = q_gain.shape[0]
    n_heads = w_q.shape[1] // head_dim
    n_kv = w_k.shape[1] // head_dim
    h_f32 = hidden.astype(jnp.float32)
    x_norm = rms_scale(h_f32, ln_attn).astype(jnp.bfloat16)
    q_proj = jnp.dot(x_norm, w_q, preferred_element_type=jnp.float32).reshape(n_seq, n_heads, head_dim)
    k_proj = jnp.dot(x_norm, w_k, preferred_element_type=jnp.float32).reshape(n_seq, n_kv, head_dim)
    v_new = jnp.dot(x_norm, w_v, preferred_element_type=jnp.float32).astype(jnp.bfloat16).reshape(n_seq, n_kv, head_dim)
    inv_freq = jnp.power(ROPE_BASE, -jnp.arange(0, head_dim, 2).astype(jnp.float32) / head_dim)
    angles = seq_lens.astype(jnp.float32)[:, None, None] * inv_freq[None, None, :]
    q_rot = rotate_half(rms_scale(q_proj, q_gain), angles).astype(jnp.bfloat16)
    k_new = rotate_half(rms_scale(k_proj, k_gain), angles).astype(jnp.bfloat16)
    positions = jnp.arange(t_max, dtype=jnp.int32)
    at_slot = (positions[None, :] == seq_lens[:, None])[:, :, None, None]
    k_all = jnp.where(at_slot, k_new[:, None], k_cache)
    v_all = jnp.where(at_slot, v_new[:, None], v_cache)
    q_grp = q_rot.reshape(n_seq, n_kv, n_heads // n_kv, head_dim)
    scores = jnp.einsum('skgd,stkd->skgt', q_grp, k_all, preferred_element_type=jnp.float32) * (head_dim ** -0.5)
    visible = (positions[None, :] <= seq_lens[:, None])[:, None, None, :]
    scores = jnp.where(visible, scores, -1e30)
    att_probs = jax.nn.softmax(scores, axis=-1).astype(jnp.bfloat16)
    attn_out = jnp.einsum('skgt,stkd->skgd', att_probs, v_all, preferred_element_type=jnp.float32)
    attn_out = attn_out.astype(jnp.bfloat16).reshape(n_seq, n_heads * head_dim)
    y_res = h_f32 + jnp.dot(attn_out, w_o, preferred_element_type=jnp.float32)
    return y_res, k_all, v_all


def route_tables(expert_ids, n_experts, capacity):
    expert_range = jnp.arange(n_experts, dtype=jnp.int32)
    chosen = jnp.any(expert_ids[:, :, None] == expert_range, axis=1)
    chosen_int = chosen.astype(jnp.int32)
    rank_se = jnp.cumsum(chosen_int, axis=0) - chosen_int
    cap_range = jnp.arange(capacity, dtype=jnp.int32)
    send_map = (rank_se.T[:, None, :] == cap_range[None, :, None]) & chosen.T[:, None, :]
    slot_rank = jnp.take_along_axis(rank_se, expert_ids, axis=1)
    slot_ids = expert_ids * capacity + slot_rank
    return send_map.astype(jnp.bfloat16), slot_ids


def solution(mesh):
    n_group = mesh.shape['ep']
    row_spec = P(('dp', 'ep'), None)
    cache_spec = P(('dp', 'ep'), None, None, None)
    len_spec = P(('dp', 'ep'))
    rep_vec = P(None)
    rep_mat = P(None, None)
    exp_spec = P('ep', None, None)

    def local_step(hidden, k_cache, v_cache, seq_lens, expert_ids, ln_attn, w_q, w_k, w_v, q_gain, k_gain, w_o, ln_moe, w_router, w_gate, w_up, w_down):
        y_res, k_all, v_all = attend(hidden, k_cache, v_cache, seq_lens, ln_attn, w_q, w_k, w_v, q_gain, k_gain, w_o)
        r_norm = rms_scale(y_res, ln_moe).astype(jnp.bfloat16)
        logits = jnp.dot(r_norm, w_router, preferred_element_type=jnp.float32)
        gate_vals = jax.nn.softmax(jnp.take_along_axis(logits, expert_ids, axis=1), axis=-1)
        n_seq, n_top = expert_ids.shape
        n_experts = w_router.shape[1]
        n_local = w_gate.shape[0]
        capacity = 2 * n_seq // (n_experts // n_top)
        send_map, slot_ids = route_tables(expert_ids, n_experts, capacity)
        send_rows = jnp.einsum('ecs,sd->ecd', send_map, r_norm, preferred_element_type=jnp.float32).astype(jnp.bfloat16)
        recv_rows = lax.all_to_all(send_rows, 'ep', 0, 0, tiled=True)
        recv_rows = recv_rows.reshape(n_group, n_local, capacity, -1)
        gate_pre = jnp.einsum('secd,edf->secf', recv_rows, w_gate, preferred_element_type=jnp.float32)
        up_pre = jnp.einsum('secd,edf->secf', recv_rows, w_up, preferred_element_type=jnp.float32)
        hidden_act = (jax.nn.silu(gate_pre) * up_pre).astype(jnp.bfloat16)
        out_rows = jnp.einsum('secf,efd->secd', hidden_act, w_down, preferred_element_type=jnp.float32).astype(jnp.bfloat16)
        back_rows = lax.all_to_all(out_rows.reshape(n_group * n_local, capacity, -1), 'ep', 0, 0, tiled=True)
        picked = jnp.take(back_rows.reshape(n_experts * capacity, -1), slot_ids.reshape(-1), axis=0)
        picked = picked.reshape(n_seq, n_top, -1).astype(jnp.float32)
        moe_out = jnp.sum(gate_vals[:, :, None] * picked, axis=1)
        return (y_res + moe_out).astype(jnp.bfloat16), k_all, v_all

    return jax.shard_map(local_step, mesh=mesh, in_specs=(row_spec, cache_spec, cache_spec, len_spec, row_spec, rep_vec, rep_mat, rep_mat, rep_mat, rep_vec, rep_vec, rep_mat, rep_vec, rep_mat, exp_spec, exp_spec, exp_spec), out_specs=(row_spec, cache_spec, cache_spec), check_vma=False)
```

profile of v0, /device:TPU:21, one launch (start us, length us, event | category | flops | bytes accessed | tf_op | source)
XLA Modules:
  0.0 303.6 jit_solution(11652802505213388185)
XLA Ops:
  0.7 0.8 convert_element_type.76
  2.9 1.1 fusion.24
  4.0 1.9 multiply_reduce_fusion.3
  6.6 1.7 convolution_convert_fusion.2
  8.8 7.6 %broadcast_select_fusion.1 = (bf16[128,32,8,64]{0,3,2,1:T(8,128)(2,1)}, bf16[128,32,8,64]{0,3,2,1:T(8,128)(2,1)}) fusion(bf16[128,32,8,64]{0,3,2,1:T(8,128)(2,1)} %param.18, pred[128,32]{0,1:T(8,128)(4,1)S(1)} %copy.78, bf16[128,8,64]{0,2,1:T(8,128)(2,1)S(1)} %pad_maximum_fusion, bf16[128,32,8,64]{0,3,2,1:T(8,128)(2,1)} %param.19, ...), kind=kLoop, calls=%fused_computation.14 | loop fusion | flops 4194304 | bytes 17043456 | tf_op jit(solution)/shard_map/jit(_where)/select_n | solution.py:41
  16.4 13.0 %copy.80 = bf16[128,32,8,64]{3,1,2,0:T(8,128)(2,1)} copy(bf16[128,32,8,64]{0,3,2,1:T(8,128)(2,1)} %get-tuple-element.10) | data formatting | bytes 8388608 | tf_op jit(solution)/shard_map/jit(_where)/select_n | solution.py:41
  29.5 2.6 multiply_reduce_fusion.2
  32.7 1.2 copy.77
  33.9 13.0 %copy.82 = bf16[128,32,8,64]{3,1,2,0:T(8,128)(2,1)} copy(bf16[128,32,8,64]{0,3,2,1:T(8,128)(2,1)} %get-tuple-element.11) | data formatting | bytes 8388608 | tf_op jit(solution)/shard_map/jit(_where)/select_n | solution.py:42
  47.0 9.0 %fusion.46 = (f32[128,8,2]{2,1,0:T(8,128)}, f32[128,8,2,32]{3,2,1,0:T(2,128)}) fusion(bf16[128,32,8,64]{3,1,2,0:T(8,128)(2,1)} %copy.80, pred[128,32]{1,0:T(8,128)(4,1)S(1)} %get-tuple-element.14, bf16[128,8,2,32]{3,2,1,0:T(2,128)(2,1)S(1)} %bitcast.80, bf16[128,8,2,32]{3,2,1,0:T(2,128)(2,1)S(1)} %bitcast.79), kind=kOutput, calls=%fused_computation.90 | convolution fusion | flops 9175071 | bytes 4730880 | tf_op jit(solution)/shard_map/sub | solution.py:47
  56.0 6.3 %convolution_convert_fusion.1 = bf16[128,8,2,64]{3,2,1,0:T(2,128)(2,1)S(1)} fusion(bf16[128,32,8,64]{3,1,2,0:T(8,128)(2,1)} %copy.82, f32[128,8,2,32]{3,2,1,0:T(2,128)} %get-tuple-element.21, f32[128,8,2]{2,1,0:T(8,128)} %get-tuple-element.20), kind=kOutput, calls=%fused_computation.29 | convolution fusion | flops 8650752 | bytes 4726784 | tf_op jit(solution)/shard_map/skgt,stkd->skgd/dot_general | solution.py:48
  62.7 2.1 multiply_reduce_fusion.1
  65.3 1.3 convolution_convert_fusion
  66.7 106.3 %all_to_all.10 = bf16[32,64,1024]{2,1,0:T(8,128)(2,1)S(1)} all-to-all(bf16[32,64,1024]{2,1,0:T(8,128)(2,1)S(1)} %convolution_convert_fusion), channel_id=1, replica_groups=mesh['dp'=4,'ep'=16] {'ep'}, dimensions={0} | all-to-all | bytes 8388608 | tf_op jit(solution)/shard_map/all_to_all | solution.py:86
  173.0 2.0 copy-done.3
  175.0 4.3 %fusion.5 = f32[2,16,64,512]{3,2,1,0:T(8,128)} fusion(bf16[16,2,64,1024]{3,2,1,0:T(8,128)(2,1)S(1)} %bitcast.75, bf16[2,1024,512]{2,1,0:T(8,128)(2,1)S(1)} %copy-done.8), kind=kOutput, calls=%fused_computation.15 | convolution fusion | flops 2147483648 | bytes 10485760 | tf_op jit(solution)/shard_map/secd,edf->secf/dot_general | solution.py:89
  179.3 8.9 %convert_bitcast_fusion = bf16[16,2,64,1024]{3,2,0,1:T(8,128)(2,1)} fusion(f32[2,16,64,512]{3,2,1,0:T(8,128)} %fusion.5, bf16[16,2,64,1024]{3,2,1,0:T(8,128)(2,1)} %bitcast.76, bf16[2,512,1024]{2,1,0:T(8,128)(2,1)S(1)} %copy-done, bf16[2,1024,512]{2,1,0:T(8,128)(2,1)} %param.31), kind=kOutput, calls=%fused_computation.12 | convolution fusion | flops 4303355904 | bytes 16777216 | tf_op jit(solution)/shard_map/secf,efd->secd/dot_general | solution.py:91
  188.2 4.9 %copy.93 = bf16[16,2,64,1024]{3,2,1,0:T(8,128)(2,1)} copy(bf16[16,2,64,1024]{3,2,0,1:T(8,128)(2,1)} %convert_bitcast_fusion) | data formatting | bytes 8388608 | tf_op jit(solution)/shard_map/convert_element_type | solution.py:91
  193.0 4.8 %all-to-all-start.1 = ((bf16[32,64,1024]{2,1,0:T(8,128)(2,1)}), bf16[32,64,1024]{2,1,0:T(8,128)(2,1)}, u32[]{:S(2)}, u32[]{:S(2)}) async-start(bf16[32,64,1024]{2,1,0:T(8,128)(2,1)} %bitcast.74), calls=%async_computation.1 | async-start | bytes 8388608 | tf_op jit(solution)/shard_map/all_to_all | solution.py:92
  198.3 7.0 %gather_fusion.1 = f32[1024]{0:T(1024)S(1)} fusion(f32[128,32]{0,1:T(8,128)S(1)} %fusion.40, s32[1024]{0:T(1024)S(1)} %reshape.274), kind=kCustom, calls=%fused_computation.1 | custom fusion | bytes 16384 | tf_op jit(solution)/shard_map/jit(take_along_axis)/gather | solution.py:79
  205.5 7.1 %gather_fusion.2 = s32[1024]{0:T(1024)S(1)} fusion(s32[128,32]{1,0:T(8,128)S(1)} %convert_subtract_fusion, s32[1024]{0:T(1024)S(1)} %reshape.274), kind=kCustom, calls=%fused_computation.2 | custom fusion | bytes 16384 | tf_op jit(solution)/shard_map/jit(take_along_axis)/gather | solution.py:61
  213.3 77.5 %all-to-all-done.1 = bf16[32,64,1024]{2,1,0:T(8,128)(2,1)} async-done(((bf16[32,64,1024]{2,1,0:T(8,128)(2,1)}), bf16[32,64,1024]{2,1,0:T(8,128)(2,1)}, u32[]{:S(2)}, u32[]{:S(2)}) %all-to-all-start.1) | async-done | bytes 4194336 | tf_op jit(solution)/shard_map/all_to_all | solution.py:92
  290.8 8.9 %gather_fusion = bf16[1024,1024]{1,0:T(8,128)(2,1)} fusion(bf16[2048,1024]{1,0:T(8,128)(2,1)} %bitcast.21, s32[1024]{0:T(1024)S(1)} %broadcast_clamp_fusion), kind=kCustom, calls=%fused_computation | custom fusion | bytes 4198400 | tf_op jit(solution)/shard_map/jit(_take)/gather | solution.py:93
  299.7 3.1 %multiply_reduce_fusion = f32[128,1024]{1,0:T(8,128)S(1)} fusion(bf16[1024,1024]{1,0:T(8,128)(2,1)} %gather_fusion, f32[128,8]{1,0:T(8,128)S(1)} %copy.86, pred[128,8]{1,0:T(8,128)(4,1)S(1)} %copy.89), kind=kLoop, calls=%fused_computation.11 | loop fusion | flops 4063232 | bytes 2626560 | tf_op jit(solution)/shard_map/reduce_sum | solution.py:95
  (65 shorter events, 6.2 us)
Async XLA Ops:
  0.6 178.7 %copy-start = (bf16[2,512,1024]{2,1,0:T(8,128)(2,1)S(1)}, bf16[2,512,1024]{2,1,0:T(8,128)(2,1)}, u32[]{:S(2)}) copy-start(bf16[2,512,1024]{2,1,0:T(8,128)(2,1)} %param.33) | copy-start | bytes 6291460
  16.4 13.0 %copy-start.2 = (bf16[128,1024]{1,0:T(8,128)(2,1)S(1)}, bf16[128,1024]{1,0:T(8,128)(2,1)}, u32[]{:S(2)}) copy-start(bf16[128,1024]{1,0:T(8,128)(2,1)} %param.17) | copy-start | bytes 786436
  16.4 15.6 %copy-start.9 = (bf16[64]{0:T(256)(128)(2,1)S(1)}, bf16[64]{0:T(256)(128)(2,1)}, u32[]{:S(2)}) copy-start(bf16[64]{0:T(256)(128)(2,1)} %param.26) | copy-start | bytes 388
  33.9 13.0 %copy-start.4 = (bf16[128,16,32]{2,1,0:T(8,128)(2,1)S(1)}, bf16[128,16,32]{2,1,0:T(8,128)(2,1)}, u32[]{:S(2)}) copy-start(bf16[128,16,32]{2,1,0:T(8,128)(2,1)} %copy.77) | copy-start | bytes 393220
  56.0 8.9 %copy-start.7 = (bf16[1024]{0:T(1024)(128)(2,1)S(1)}, bf16[1024]{0:T(1024)(128)(2,1)}, u32[]{:S(2)}) copy-start(bf16[1024]{0:T(1024)(128)(2,1)} %param.29) | copy-start | bytes 6148
  56.0 8.9 %copy-start.6 = (s32[128,8]{0,1:T(8,128)S(1)}, s32[128,8]{0,1:T(8,128)}, u32[]{:S(2)}) copy-start(s32[128,8]{0,1:T(8,128)} %param.21) | copy-start | bytes 12292
  66.7 108.3 %copy-start.8 = (bf16[2,1024,512]{2,1,0:T(8,128)(2,1)S(1)}, bf16[2,1024,512]{2,1,0:T(8,128)(2,1)}, u32[]{:S(2)}) copy-start(bf16[2,1024,512]{2,1,0:T(8,128)(2,1)} %param.32) | copy-start | bytes 6291460
  173.0 2.0 copy-start.3
  193.0 5.0 %copy-start.5 = (bf16[1024,32]{0,1:T(8,128)(2,1)S(1)}, bf16[1024,32]{0,1:T(8,128)(2,1)}, u32[]{:S(2)}) copy-start(bf16[1024,32]{0,1:T(8,128)(2,1)} %param.30) | copy-start | bytes 196612
  193.0 97.7 %all-to-all-start.1 = ((bf16[32,64,1024]{2,1,0:T(8,128)(2,1)}), bf16[32,64,1024]{2,1,0:T(8,128)(2,1)}, u32[]{:S(2)}, u32[]{:S(2)}) async-start(bf16[32,64,1024]{2,1,0:T(8,128)(2,1)} %bitcast.74), calls=%async_computation.1 | async-start | bytes 8388608 | tf_op jit(solution)/shard_map/all_to_all | solution.py:92
  290.8 12.8 %copy-start.1 = (bf16[2,512,1024]{2,1,0:T(8,128)(2,1)S(1)}, bf16[2,512,1024]{2,1,0:T(8,128)(2,1)}, u32[]{:S(2)}) copy-start(bf16[2,512,1024]{2,1,0:T(8,128)(2,1)} %param.33) | copy-start | bytes 6291460
where the time goes:
time: 305 us; the launch traced here: 304 us
  blocking collectives  106 us (35%)
  waiting for transfers between devices  77.5 us (25%)
  local copies, waits for them, and re-layouts  59.4 us (19%)
  matrix products  38.3 us (13%)
  other arithmetic  16.4 us (5%)
  starting transfers between devices  4.78 us (2%)
    all_to_all x1, blocking collectives, local_step(): recv_rows = lax.all_to_all(send_rows, 'ep', 0, 0, tiled=True)  106 us
    all_to_all x1, waiting for transfers between devices, local_step(): lax.all_to_all(out_rows.reshape(n_group * n_local, capacity, -1), 'ep', 0...  77.5 us
    select_n x1, local copies, waits for them, and re-layouts, attend(): k_all = jnp.where(at_slot, k_new[:, None], k_cache)  13 us
    select_n x1, local copies, waits for them, and re-layouts, attend(): v_all = jnp.where(at_slot, v_new[:, None], v_cache)  13 us
    sub x1, matrix products, attend(): att_probs = jax.nn.softmax(scores, axis=-1).astype(jnp.bfloat16)  9.04 us
    gather x1, local copies, waits for them, and re-layouts, local_step(): jnp.take(back_rows.reshape(n_experts * capacity, -1), slot_ids.reshape(-1...  8.93 us
    dot_general x1, matrix products, local_step(): jnp.einsum('secf,efd->secd', hidden_act, w_down, preferred_element_type=j...  8.85 us
    select_n x1, other arithmetic, attend(): k_all = jnp.where(at_slot, k_new[:, None], k_cache)  7.63 us
  transfers between devices with their start and end apart: 1, of which 1 were waited for; matrix products, arithmetic and copies ran while one was open for 5% of the time, Pallas kernels for 0%

commit v1 on v0

v1 whole, which is shorter than its diff:
```python
import functools

import jax
import jax.numpy as jnp
import numpy as np
from jax import lax
from jax.experimental import pallas as pl
from jax.experimental.pallas import tpu as pltpu
from jax.sharding import PartitionSpec as P

EPS = 1e-6
ROPE_BASE = 1000000.0
F32 = jnp.float32
BF16 = jnp.bfloat16
MESH = pl.DeviceIdType.MESH


def attend_kernel(h_ref, lens_ref, ids_ref, ln_a_ref, qg_ref, kg_ref, ln_m_ref, freq_ref, wr_ref,
                  wq_hbm, wk_hbm, wv_hbm, wo_hbm, kc_hbm, vc_hbm,
                  kn_hbm, vn_hbm, y_ref, r_ref, gate_ref,
                  kbuf, vbuf, wq, wk, wv, wo, qrot, knew, vnew, score, attn, in_sem, out_sem):
    t_max, n_kv, hd, n_seq = kc_hbm.shape
    n_heads = wq_hbm.shape[1] // hd
    grp = n_heads // n_kv
    half = hd // 2
    n_chunk = 4
    tc = t_max // n_chunk

    w_copies = [pltpu.make_async_copy(src, dst, in_sem.at[i])
                for i, (src, dst) in enumerate(((wk_hbm, wk), (wq_hbm, wq), (wv_hbm, wv), (wo_hbm, wo)))]
    k_in = [pltpu.make_async_copy(kc_hbm.at[pl.ds(c * tc, tc)], kbuf.at[pl.ds(c * tc, tc)], in_sem.at[4 + c]) for c in range(n_chunk)]
    v_in = [pltpu.make_async_copy(vc_hbm.at[pl.ds(c * tc, tc)], vbuf.at[pl.ds(c * tc, tc)], in_sem.at[4 + n_chunk + c]) for c in range(n_chunk)]
    k_out = [pltpu.make_async_copy(kbuf.at[pl.ds(c * tc, tc)], kn_hbm.at[pl.ds(c * tc, tc)], out_sem.at[c]) for c in range(n_chunk)]
    v_out = [pltpu.make_async_copy(vbuf.at[pl.ds(c * tc, tc)], vn_hbm.at[pl.ds(c * tc, tc)], out_sem.at[n_chunk + c]) for c in range(n_chunk)]
    for copy in w_copies[:3] + k_in + v_in + w_copies[3:]:
        copy.start()

    h32 = h_ref[...].astype(F32)
    mean_sq = jnp.mean(h32 * h32, axis=1, keepdims=True)
    x = (h32 * lax.rsqrt(mean_sq + EPS) * ln_a_ref[...].astype(F32)).astype(BF16)

    lens = lens_ref[...]
    angles = lens.astype(F32) * freq_ref[...]
    cos_v = jnp.cos(angles)
    sin_v = jnp.sin(angles)

    def gain_tile(g_ref):
        row = g_ref[...].astype(F32)
        row = jnp.concatenate([row] * (n_seq // hd), axis=1)
        return jnp.transpose(jnp.broadcast_to(row, (n_seq, n_seq)))[:hd, :]

    def rope_heads(proj, gain, dst, heads):
        for i in range(heads):
            if i % 2 == 0:
                pair = jnp.transpose(proj[:, i * hd:(i + 2) * hd])
            vals = pair[(i % 2) * hd:(i % 2 + 1) * hd, :]
            ms = jnp.mean(vals * vals, axis=0, keepdims=True)
            vals = vals * lax.rsqrt(ms + EPS) * gain
            low, high = vals[:half, :], vals[half:, :]
            dst[i * hd:i * hd + half, :] = (low * cos_v - high * sin_v).astype(BF16).astype(F32)
            dst[i * hd + half:(i + 1) * hd, :] = (high * cos_v + low * sin_v).astype(BF16).astype(F32)

    w_copies[0].wait()
    rope_heads(jnp.dot(x, wk[...], preferred_element_type=F32), gain_tile(kg_ref), knew, n_kv)
    w_copies[1].wait()
    rope_heads(jnp.dot(x, wq[...], preferred_element_type=F32), gain_tile(qg_ref), qrot, n_heads)
    w_copies[2].wait()
    v_proj = jnp.dot(x, wv[...], preferred_element_type=F32)
    for i in range(0, n_kv, 2):
        vnew[i * hd:(i + 2) * hd, :] = jnp.transpose(v_proj[:, i * hd:(i + 2) * hd]).astype(BF16).astype(F32)

    for c in range(n_chunk):
        k_in[c].wait()

        def k_body(kv, carry, c=c):
            new = knew[pl.ds(pl.multiple_of(kv * hd, hd), hd), :]
            qs = [qrot[pl.ds(pl.multiple_of((kv * grp + g) * hd, hd), hd), :] for g in range(grp)]
            rows = [[] for _ in range(grp)]
            for tt in range(tc):
                t = c * tc + tt
                kt = jnp.where(lens == t, new, kbuf[t, kv].astype(F32))
                kbuf[t, kv] = kt.astype(BF16)
                for g in range(grp):
                    rows[g].append(jnp.sum(kt * qs[g], axis=0, keepdims=True))
            for g in range(grp):
                score[kv * grp + g, c * tc:(c + 1) * tc, :] = jnp.concatenate(rows[g], axis=0)
            return carry

        lax.fori_loop(0, n_kv, k_body, 0)
        k_out[c].start()

    visible = lax.broadcasted_iota(jnp.int32, (t_max, n_seq), 0) <= lens

    def soft_body(j, carry):
        s = jnp.where(visible, score[j] * (hd ** -0.5), -1e30)
        e = jnp.exp(s - jnp.max(s, axis=0, keepdims=True))
        score[j] = (e / jnp.sum(e, axis=0, keepdims=True)).astype(BF16).astype(F32)
        return carry

    lax.fori_loop(0, n_heads, soft_body, 0, unroll=2)

    for c in range(n_chunk):
        v_in[c].wait()

        def v_body(kv, carry, c=c):
            new = vnew[pl.ds(pl.multiple_of(kv * hd, hd), hd), :]
            at = [pl.ds(pl.multiple_of((kv * grp + g) * hd, hd), hd) for g in range(grp)]
            acc = [None if c == 0 else attn[at[g], :] for g in range(grp)]
            for tt in range(tc):
                t = c * tc + tt
                vt = jnp.where(lens == t, new, vbuf[t, kv].astype(F32))
                vbuf[t, kv] = vt.astype(BF16)
                for g in range(grp):
                    term = vt * score[kv * grp + g, t:t + 1, :]
                    acc[g] = term if acc[g] is None else acc[g] + term
            for g in range(grp):
                attn[at[g], :] = acc[g]
            return carry

        lax.fori_loop(0, n_kv, v_body, 0)
        v_out[c].start()

    w_copies[3].wait()
    a_rows = jnp.concatenate([jnp.transpose(attn[i * n_seq:(i + 1) * n_seq, :]).astype(BF16) for i in range(n_heads * hd // n_seq)], axis=1)
    y = h32 + jnp.dot(a_rows, wo[...], preferred_element_type=F32)
    y_ref[...] = y
    mean_sq = jnp.mean(y * y, axis=1, keepdims=True)
    r = (y * lax.rsqrt(mean_sq + EPS) * ln_m_ref[...].astype(F32)).astype(BF16)
    r_ref[...] = r
    logits = lax.dot_general(wr_ref[...], r, (((1,), (1,)), ((), ())), preferred_element_type=F32)
    e_iota = lax.broadcasted_iota(jnp.int32, logits.shape, 0)
    ids = ids_ref[...]
    chosen = e_iota == ids[0:1, :]
    for i in range(1, ids.shape[0]):
        chosen = chosen | (e_iota == ids[i:i + 1, :])
    top = jnp.max(jnp.where(chosen, logits, -jnp.inf), axis=0, keepdims=True)
    e = jnp.where(chosen, jnp.exp(logits - top), 0.0)
    gate_ref[...] = jnp.where(chosen, e / jnp.sum(e, axis=0, keepdims=True), -1.0)

    for copy in k_out + v_out:
        copy.wait()


def attend(hidden, k_t, v_t, lens, ids_t, ln_attn, w_q, w_k, w_v, q_gain, k_gain, w_o, ln_moe, w_router_t):
    n_seq, d = hidden.shape
    t_max, n_kv, hd, _ = k_t.shape
    hq, hk = w_q.shape[1], w_k.shape[1]
    n_heads = hq // hd
    n_exp = w_router_t.shape[0]
    freq = np.power(ROPE_BASE, -np.arange(0, hd, 2).astype(np.float32) / hd).astype(np.float32)
    freq = jnp.asarray(np.broadcast_to(freq[:, None], (hd // 2, n_seq)))
    vm = pl.BlockSpec(memory_space=pltpu.VMEM)
    anyspace = pl.BlockSpec(memory_space=pl.ANY)
    return pl.pallas_call(
        attend_kernel,
        out_shape=(
            jax.ShapeDtypeStruct(k_t.shape, k_t.dtype),
            jax.ShapeDtypeStruct(v_t.shape, v_t.dtype),
            jax.ShapeDtypeStruct((n_seq, d), F32),
            jax.ShapeDtypeStruct((n_seq, d), BF16),
            jax.ShapeDtypeStruct((n_exp, n_seq), F32),
        ),
        in_specs=[vm] * 9 + [anyspace] * 6,
        out_specs=(anyspace, anyspace, vm, vm, vm),
        scratch_shapes=[
            pltpu.VMEM(k_t.shape, BF16), pltpu.VMEM(v_t.shape, BF16),
            pltpu.VMEM(w_q.shape, BF16), pltpu.VMEM(w_k.shape, BF16), pltpu.VMEM(w_v.shape, BF16), pltpu.VMEM(w_o.shape, BF16),
            pltpu.VMEM((hq, n_seq), F32), pltpu.VMEM((hk, n_seq), F32), pltpu.VMEM((hk, n_seq), F32),
            pltpu.VMEM((n_heads, t_max, n_seq), F32), pltpu.VMEM((hq, n_seq), F32),
            pltpu.SemaphoreType.DMA((12,)), pltpu.SemaphoreType.DMA((8,)),
        ],
        compiler_params=pltpu.CompilerParams(vmem_limit_bytes=30 * 1024 * 1024),
        name="attend",
    )(hidden, lens, ids_t, ln_attn, q_gain, k_gain, ln_moe, freq, w_router_t, w_q, w_k, w_v, w_o, k_t, v_t)


def moe_kernel(n, r_ref, gate_ref, y_ref, wg_hbm, wu_hbm, wd_hbm, out_ref,
               xbuf, gbuf, cboth, cpart, inc, wg, wu, wd, act, gcol,
               w_sem, own_sem, ring_send, ring_recv, gate_send, gate_recv,
               pair_send, pair_recv, pgate_send, pgate_recv, self_send, self_recv,
               sum_send, sum_recv, rs_send, rs_recv):
    me = lax.axis_index("ep")
    chip = me // 2
    core = lax.rem(me, 2)
    other = 1 - core
    half = n // 2
    n_unit = n - 1
    rows, d = r_ref.shape
    n_local = wg_hbm.shape[0]
    hr = rows // 2
    qr = hr // 2

    def at_chip(step):
        return lax.rem(chip + step + n, n)

    def ring_dev(direction):
        return {"ep": 2 * at_chip(1 if direction == 0 else -1) + core}

    pair_dev = {"ep": 2 * chip + other}

    def remote(src, dst, ssem, rsem, dev):
        return pltpu.make_async_remote_copy(src_ref=src, dst_ref=dst, send_sem=ssem, recv_sem=rsem, device_id=dev, device_id_type=MESH)

    barrier = pltpu.get_barrier_semaphore()
    for dev in (ring_dev(0), ring_dev(1), pair_dev):
        pl.semaphore_signal(barrier, inc=1, device_id=dev, device_id_type=MESH)

    w_copies = [pltpu.make_async_copy(src, dst, w_sem.at[i]) for i, (src, dst) in enumerate(((wg_hbm, wg), (wu_hbm, wu), (wd_hbm, wd)))]
    own_copies = [pltpu.make_async_copy(r_ref, xbuf.at[chip, core], own_sem.at[0]),
                  pltpu.make_async_copy(gate_ref, gbuf.at[chip, core], own_sem.at[1])]
    for copy in own_copies + w_copies:
        copy.start()
    for copy in own_copies:
        copy.wait()
    pl.semaphore_wait(barrier, 3)

    def unit_half(direction, u):
        return u % 2 if direction == 0 else 1 - u % 2

    def unit_from(direction, u):
        s = u // 2 + 1
        return at_chip(-s if direction == 0 else s)

    def has_gate(direction, u):
        return u % 2 == 0 and (direction == 0 or u < n_unit - 1)

    def x_at(i, c, direction, u):
        return xbuf.at[i, c, pl.ds(unit_half(direction, u) * hr, hr)]

    def ring_copy(direction, u, i):
        ref = x_at(i, core, direction, u)
        return remote(ref, ref, ring_send.at[direction, u], ring_recv.at[direction, u], ring_dev(direction))

    def ring_gate(direction, u, i):
        ref = gbuf.at[i, core]
        return remote(ref, ref, gate_send.at[direction, u // 2], gate_recv.at[direction, u // 2], ring_dev(direction))

    def pair_copy(direction, u, i, c):
        ref = x_at(i, c, direction, u)
        return remote(ref, ref, pair_send.at[direction, u], pair_recv.at[direction, u], pair_dev)

    def pair_gate(direction, u, i, c):
        ref = gbuf.at[i, c]
        return remote(ref, ref, pgate_send.at[direction, u // 2], pgate_recv.at[direction, u // 2], pair_dev)

    def self_copies(c):
        return [remote(xbuf.at[chip, c], xbuf.at[chip, c], self_send.at[0], self_recv.at[0], pair_dev),
                remote(gbuf.at[chip, c], gbuf.at[chip, c], self_send.at[1], self_recv.at[1], pair_dev)]

    def send_chip(direction, u):
        s = u // 2
        return at_chip(-s if direction == 0 else s)

    def start_unit(direction, u):
        i = send_chip(direction, u)
        if has_gate(direction, u):
            ring_gate(direction, u, i).start()
        ring_copy(direction, u, i).start()

    for u in range(2):
        for direction in range(2):
            start_unit(direction, u)
        if u == 0:
            for copy in self_copies(core):
                copy.start()

    def take_unit(u):
        for direction in range(2):
            i = unit_from(direction, u)
            if has_gate(direction, u):
                ring_gate(direction, u, i).wait_recv()
            ring_copy(direction, u, i).wait_recv()
            if u + 2 < n_unit:
                start_unit(direction, u + 2)
            if has_gate(direction, u):
                pair_gate(direction, u, i, core).start()
            pair_copy(direction, u, i, core).start()

    def wait_pair(direction, u):
        i = unit_from(direction, u)
        if has_gate(direction, u):
            pair_gate(direction, u, i, other).wait_recv()
        pair_copy(direction, u, i, other).wait_recv()

    def sum_copy(k, i):
        return remote(cboth.at[i, other], cpart.at[i], sum_send.at[k], sum_recv.at[k], pair_dev)

    def order_step(k):
        return 0 if k == 0 else (-((k + 1) // 2) if k % 2 == 1 and k < n - 1 else (k + 1) // 2)

    order = [order_step(k) for k in range(n)]

    def rs_list(direction):
        lh, sh = (0, 1) if direction == 0 else (1, 0)
        seq = [(half - 1, sh, 0), (half, lh, 0), (half, lh, 1), (half - 1, sh, 1)]
        for q in range(half - 1, 0, -1):
            seq += [(q, lh, 0), (q, lh, 1)]
            if q > 1:
                seq += [(q - 1, sh, 0), (q - 1, sh, 1)]
        return seq

    rs_lists = [rs_list(0), rs_list(1)]

    def rs_copy(direction, u):
        q, h, p = rs_lists[direction][u]
        t = at_chip(q if direction == 0 else -q)
        at = pl.ds(h * hr + p * qr, qr)
        return remote(cboth.at[t, core, at], inc.at[direction, q - 1, at], rs_send.at[direction, u], rs_recv.at[direction, u], ring_dev(direction))

    def rs_step(direction, u):
        q, h, p = rs_lists[direction][u]
        step = q if direction == 0 else -q
        t = at_chip(step)
        at = pl.ds(h * hr + p * qr, qr)
        total = cboth[t, core, at, :] + cpart[t, at, :]
        if (q + 1, h, p) in rs_lists[direction]:
            rs_copy(direction, rs_lists[direction].index((q + 1, h, p))).wait_recv()
            total = total + inc[direction, q, at, :]
        cboth[t, core, at, :] = total
        rs_copy(direction, u).start()

    def wait_sum(step):
        step = step if step in order else step + n if step + n in order else step - n
        k = order.index(step)
        sum_copy(k, at_chip(step)).wait_recv()

    def before(k):
        if k == 0:
            for copy in self_copies(other):
                copy.wait_recv()
            for copy in w_copies:
                copy.wait()
            return
        if k == 1:
            take_unit(0)
            take_unit(1)
        elif k < n - 2:
            take_unit(k)
        elif k == n - 1:
            take_unit(n_unit - 1)
            wait_sum(-(half - 1))
            rs_step(1, 0)
            wait_sum(half - 1)
            rs_step(0, 0)
            wait_pair(0, n_unit - 1)
            wait_pair(1, n_unit - 1)
            return
        direction = 0 if order[k] < 0 else 1
        s = abs(order[k]) - 1
        wait_pair(direction, 2 * s)
        wait_pair(direction, 2 * s + 1)

    def compute(i):
        x = xbuf[i].reshape(2 * rows, d)
        for e in range(n_local):
            for c in range(2):
                row = gbuf[i, c, pl.ds(n_local * me + e, 1), :]
                gcol[e, c * rows:(c + 1) * rows, :] = jnp.transpose(jnp.broadcast_to(row, (rows, rows)))
        ft = 256
        for e in range(n_local):
            for nt in range(wg.shape[2] // ft):
                cols = slice(nt * ft, (nt + 1) * ft)
                g = jnp.dot(x, wg[e, :, cols], preferred_element_type=F32)
                u = jnp.dot(x, wu[e, :, cols], preferred_element_type=F32)
                act[:, cols] = (jax.nn.silu(g) * u).astype(BF16)
            a = act[...]
            gc = gcol[e]
            chosen = gc >= 0.0
            for nt in range(d // ft):
                f = jnp.dot(a, wd[e, :, nt * ft:(nt + 1) * ft], preferred_element_type=F32).astype(BF16).astype(F32)
                for l in range(ft // rows):
                    cols = slice(nt * ft + l * rows, nt * ft + (l + 1) * rows)
                    term = jnp.where(chosen, f[:, l * rows:(l + 1) * rows] * gc, 0.0).reshape(2, rows, rows)
                    cboth[i, :, :, cols] = term if e == 0 else cboth[i, :, :, cols] + term

    def body(k, carry):
        for kk in range(n):
            @pl.when(k == kk)
            def _(kk=kk):
                before(kk)
        s = (k + 1) // 2
        step = jnp.where((lax.rem(k, 2) == 1) & (k < n - 1), -s, s)
        i = at_chip(step)
        compute(i)
        sum_copy(k, i).start()
        return carry

    lax.fori_loop(0, n, body, 0)

    waited = {half - 1, -(half - 1)}
    n_rs = len(rs_lists[0])
    for u in range(1, n_rs):
        for direction in range(2):
            q = rs_lists[direction][u][0]
            step = q if direction == 0 else -q
            if step == -half:
                step = half
            if step not in waited:
                wait_sum(step)
                waited.add(step)
            rs_step(direction, u)
    wait_sum(0)
    for h in range(2):
        for p in range(2):
            at = pl.ds(h * hr + p * qr, qr)
            total = y_ref[at, :] + (cboth[chip, core, at, :] + cpart[chip, at, :])
            for direction in range(2):
                rs_copy(direction, rs_lists[direction].index((1, h, p))).wait_recv()
                total = total + inc[direction, 0, at, :]
            out_ref[at, :] = total.astype(out_ref.dtype)

    for direction in range(2):
        for u in range(n_unit):
            i = send_chip(direction, u)
            ring_copy(direction, u, i).wait_send()
            j = unit_from(direction, u)
            pair_copy(direction, u, j, core).wait_send()
            if has_gate(direction, u):
                ring_gate(direction, u, i).wait_send()
                pair_gate(direction, u, j, core).wait_send()
        for u in range(n_rs):
            rs_copy(direction, u).wait_send()
    for copy in self_copies(core):
        copy.wait_send()
    for k in range(n):
        sum_copy(k, at_chip(order[k])).wait_send()


def moe(n_ep, r, gates, y, w_gate, w_up, w_down):
    n = n_ep // 2
    rows, d = r.shape
    n_exp = gates.shape[0]
    n_local, _, ff = w_gate.shape
    vm = pl.BlockSpec(memory_space=pltpu.VMEM)
    anyspace = pl.BlockSpec(memory_space=pl.ANY)
    dma = pltpu.SemaphoreType.DMA
    n_rs = 2 * (n - 1)
    return pl.pallas_call(
        functools.partial(moe_kernel, n),
        out_shape=jax.ShapeDtypeStruct((rows, d), BF16),
        in_specs=[vm] * 3 + [anyspace] * 3,
        out_specs=vm,
        scratch_shapes=[
            pltpu.VMEM((n, 2, rows, d), BF16),
            pltpu.VMEM((n, 2, n_exp, rows), F32),
            pltpu.VMEM((n, 2, rows, d), F32),
            pltpu.VMEM((n, rows, d), F32),
            pltpu.VMEM((2, n // 2, rows, d), F32),
            pltpu.VMEM(w_gate.shape, BF16), pltpu.VMEM(w_up.shape, BF16), pltpu.VMEM(w_down.shape, BF16),
            pltpu.VMEM((2 * rows, ff), BF16),
            pltpu.VMEM((n_local, 2 * rows, rows), F32),
            dma((3,)), dma((2,)),
            dma((2, n - 1)), dma((2, n - 1)), dma((2, n // 2)), dma((2, n // 2)),
            dma((2, n - 1)), dma((2, n - 1)), dma((2, n // 2)), dma((2, n // 2)),
            dma((2,)), dma((2,)),
            dma((n,)), dma((n,)),
            dma((2, n_rs)), dma((2, n_rs)),
        ],
        compiler_params=pltpu.CompilerParams(collective_id=0, has_side_effects=True, vmem_limit_bytes=40 * 1024 * 1024),
        name="moe",
    )(r, gates, y, w_gate, w_up, w_down)


def solution(mesh):
    n_ep = mesh.shape['ep']
    row_spec = P(('dp', 'ep'), None)
    cache_spec = P(('dp', 'ep'), None, None, None)
    len_spec = P(('dp', 'ep'))
    rep_vec = P(None)
    rep_mat = P(None, None)
    exp_spec = P('ep', None, None)

    def local_step(hidden, k_cache, v_cache, seq_lens, expert_ids, ln_attn, w_q, w_k, w_v, q_gain, k_gain, w_o, ln_moe, w_router, w_gate, w_up, w_down):
        k_t = jnp.transpose(k_cache, (1, 2, 3, 0))
        v_t = jnp.transpose(v_cache, (1, 2, 3, 0))
        k_new, v_new, y, r, gates = attend(
            hidden, k_t, v_t, seq_lens[None, :], expert_ids.T, ln_attn[None, :], w_q, w_k, w_v,
            q_gain[None, :], k_gain[None, :], w_o, ln_moe[None, :], w_router.T)
        out = moe(n_ep, r, gates, y, w_gate, w_up, w_down)
        return out, jnp.transpose(k_new, (3, 0, 1, 2)), jnp.transpose(v_new, (3, 0, 1, 2))

    return jax.shard_map(local_step, mesh=mesh, in_specs=(row_spec, cache_spec, cache_spec, len_spec, row_spec, rep_vec, rep_mat, rep_mat, rep_mat, rep_vec, rep_vec, rep_mat, rep_vec, rep_mat, exp_spec, exp_spec, exp_spec), out_specs=(row_spec, cache_spec, cache_spec), check_vma=False)
```

time: 305 us -> 107 us (0.35)
  blocking collectives: 106 us -> 0 us
  Pallas kernels: 0 us -> 88.1 us
  waiting for transfers between devices: 77.5 us -> 0 us
  local copies, waits for them, and re-layouts: 59.4 us -> 17.3 us
  matrix products: 38.3 us -> 0 us
  other arithmetic: 16.4 us -> 0 us
  starting transfers between devices: 4.78 us -> 0 us
    all_to_all x1 -> x0, blocking collectives: 106 us -> none  [local_step(): recv_rows = lax.all_to_all(send_rows, 'ep', 0, 0, tiled=True)]
    pallas_call x0 -> x2, Pallas kernels: none -> 88.1 us  [the longest x1 79.5 us: moe(): pl.pallas_call(functools.partial(moe_kernel, n), out_shape=jax.ShapeDtype...]
    all_to_all x1 -> x0, waiting for transfers between devices: 77.5 us -> none  [local_step(): lax.all_to_all(out_rows.reshape(n_group * n_local, capacity, -1), 'ep', 0...]
    dot_general x9 -> x0, matrix products: 29.3 us -> none  [the longest x1 8.85 us: local_step(): jnp.einsum('secf,efd->secd', hidden_act, w_down, preferred_element_type=j...]
    select_n x2 -> x0, local copies, waits for them, and re-layouts: 26.1 us -> none  [the longest x1 13 us: attend(): k_all = jnp.where(at_slot, k_new[:, None], k_cache)]
    gather x9 -> x0, local copies, waits for them, and re-layouts: 23.5 us -> none  [the longest x1 8.93 us: local_step(): jnp.take(back_rows.reshape(n_experts * capacity, -1), slot_ids.reshape(-1...]
    unnamed x20 -> x31, local copies, waits for them, and re-layouts: 2.02 us -> 15.2 us
    sub x1 -> x0, matrix products: 9.04 us -> none  [attend(): att_probs = jax.nn.softmax(scores, axis=-1).astype(jnp.bfloat16)]
  transfers between devices with their start and end apart: 1 -> 0, of which waited for: 1 -> 0; matrix products, arithmetic and copies ran while one was open for 5% -> 0% of each run, Pallas kernels for 0% -> 0%
where the time goes in v1:
time: 107 us; the launch traced here: 106 us
  Pallas kernels  88.1 us (82%)
  local copies, waits for them, and re-layouts  17.3 us (16%)
    pallas_call x1, Pallas kernels, moe(): pl.pallas_call(functools.partial(moe_kernel, n), out_shape=jax.ShapeDtype...  79.5 us
    unnamed x31, local copies, waits for them, and re-layouts  15.2 us
    pallas_call x1, Pallas kernels, attend(): pl.pallas_call(attend_kernel, out_shape=(jax.ShapeDtypeStruct(k_t.shape,...  8.63 us

profile of v1, /device:TPU:21, one launch (start us, length us, event | category | flops | bytes accessed | tf_op | source)
XLA Modules:
  0.0 106.0 jit_solution(1482629657433798416)
XLA Ops:
  0.6 0.7 broadcast_in_dim.16.ln_a_ref
  1.3 0.7 broadcast_in_dim.19.ln_m_ref
  2.0 0.7 jit_solution_.3.freq_ref
  2.7 0.0 copy-start
  2.7 2.2 %copy-done = bf16[128,32,8,64]{0,3,2,1:T(8,128)(2,1)S(1)} copy-done((bf16[128,32,8,64]{0,3,2,1:T(8,128)(2,1)S(1)}, bf16[128,32,8,64]{0,3,2,1:T(8,128)(2,1)}, u32[]{:S(2)}) %copy-start) | copy-done | bytes 4194328
  4.9 0.0 copy-start.1
  4.9 2.2 %copy-done.1 = bf16[128,32,8,64]{0,3,2,1:T(8,128)(2,1)S(1)} copy-done((bf16[128,32,8,64]{0,3,2,1:T(8,128)(2,1)S(1)}, bf16[128,32,8,64]{0,3,2,1:T(8,128)(2,1)}, u32[]{:S(2)}) %copy-start.1) | copy-done | bytes 4194328
  7.1 0.0 copy-start.5
  7.1 1.6 %copy-done.5 = bf16[1024,1024]{1,0:T(8,128)(2,1)S(1)} copy-done((bf16[1024,1024]{1,0:T(8,128)(2,1)S(1)}, bf16[1024,1024]{1,0:T(8,128)(2,1)}, u32[]{:S(2)}) %copy-start.5) | copy-done | bytes 2097176
  8.7 1.6 %copy-done.6 = bf16[1024,1024]{1,0:T(8,128)(2,1)S(1)} copy-done((bf16[1024,1024]{1,0:T(8,128)(2,1)S(1)}, bf16[1024,1024]{1,0:T(8,128)(2,1)}, u32[]{:S(2)}) %copy-start.6) | copy-done | bytes 2097176
  10.3 1.2 %copy-done.7 = bf16[1024,512]{1,0:T(8,128)(2,1)S(1)} copy-done((bf16[1024,512]{1,0:T(8,128)(2,1)S(1)}, bf16[1024,512]{1,0:T(8,128)(2,1)}, u32[]{:S(2)}) %copy-start.7) | copy-done | bytes 1048600
  11.5 1.2 %copy-done.8 = bf16[1024,512]{1,0:T(8,128)(2,1)S(1)} copy-done((bf16[1024,512]{1,0:T(8,128)(2,1)S(1)}, bf16[1024,512]{1,0:T(8,128)(2,1)}, u32[]{:S(2)}) %copy-start.8) | copy-done | bytes 1048600
  12.7 0.9 copy-done.9
  13.7 0.8 copy-done.10
  14.5 0.7 copy-done.11
  15.2 0.7 copy-done.12
  15.9 0.7 copy-done.13
  16.5 0.7 copy-done.14
  17.2 8.6 %attend.1 = (bf16[32,8,64,128]{3,2,1,0:T(8,128)(2,1)}, bf16[32,8,64,128]{3,2,1,0:T(8,128)(2,1)}, f32[128,1024]{1,0:T(8,128)S(1)}, bf16[128,1024]{1,0:T(8,128)(2,1)S(1)}, f32[32,128]{1,0:T(8,128)S(1)}) custom-call(bf16[128,1024]{1,0:T(8,128)(2,1)S(1)} %copy-done.9, s32[1,128]{1,0:T(1,128)S(1)} %bitcast.13, s32[8,128]{1,0:T(8,128)S(1)} %bitcast.12, ...), custom_call_target="tpu_custom_call" | custom-call | tf_op jit(solution)/shard_map/attend/pallas_call | solution.py:154
  25.8 0.0 copy-done.2
  25.8 0.0 copy-done.3
  25.8 0.0 copy-done.4
  25.9 79.5 %moe.1 = bf16[128,1024]{1,0:T(8,128)(2,1)S(1)} custom-call(bf16[128,1024]{1,0:T(8,128)(2,1)S(1)} %get-tuple-element.8.r_ref, f32[32,128]{1,0:T(8,128)S(1)} %get-tuple-element.9.gate_ref, f32[128,1024]{1,0:T(8,128)S(1)} %get-tuple-element.10.y_ref, bf16[2,1024,512]{2,1,0:T(8,128)(2,1)S(1)} %copy-done.2, bf16[2,1024,512]{2,1,0:T(8,128)(2,1)S(1)} %copy-done.3, ...), custom_call_target="tpu_custom_call" | custom-call | tf_op jit(solution)/shard_map/moe/pallas_call | solution.py:438
  105.3 0.7 copy.22
  (12 shorter events, 0.0 us)
Async XLA Ops:
  2.7 2.2 %copy-start = (bf16[128,32,8,64]{0,3,2,1:T(8,128)(2,1)S(1)}, bf16[128,32,8,64]{0,3,2,1:T(8,128)(2,1)}, u32[]{:S(2)}) copy-start(bf16[128,32,8,64]{0,3,2,1:T(8,128)(2,1)} %param.19) | copy-start | bytes 12582916
  4.9 2.2 %copy-start.1 = (bf16[128,32,8,64]{0,3,2,1:T(8,128)(2,1)S(1)}, bf16[128,32,8,64]{0,3,2,1:T(8,128)(2,1)}, u32[]{:S(2)}) copy-start(bf16[128,32,8,64]{0,3,2,1:T(8,128)(2,1)} %param.20) | copy-start | bytes 12582916
  7.1 1.6 %copy-start.5 = (bf16[1024,1024]{1,0:T(8,128)(2,1)S(1)}, bf16[1024,1024]{1,0:T(8,128)(2,1)}, u32[]{:S(2)}) copy-start(bf16[1024,1024]{1,0:T(8,128)(2,1)} %wq_hbm.1) | copy-start | bytes 6291460
  8.7 1.6 %copy-start.6 = (bf16[1024,1024]{1,0:T(8,128)(2,1)S(1)}, bf16[1024,1024]{1,0:T(8,128)(2,1)}, u32[]{:S(2)}) copy-start(bf16[1024,1024]{1,0:T(8,128)(2,1)} %wo_hbm.1) | copy-start | bytes 6291460
  10.3 1.2 %copy-start.7 = (bf16[1024,512]{1,0:T(8,128)(2,1)S(1)}, bf16[1024,512]{1,0:T(8,128)(2,1)}, u32[]{:S(2)}) copy-start(bf16[1024,512]{1,0:T(8,128)(2,1)} %wk_hbm.1) | copy-start | bytes 3145732
  11.5 1.2 %copy-start.8 = (bf16[1024,512]{1,0:T(8,128)(2,1)S(1)}, bf16[1024,512]{1,0:T(8,128)(2,1)}, u32[]{:S(2)}) copy-start(bf16[1024,512]{1,0:T(8,128)(2,1)} %wv_hbm.1) | copy-start | bytes 3145732
  12.7 0.9 copy-start.9
  13.7 0.8 copy-start.10
  14.5 0.7 copy-start.11
  15.2 0.7 copy-start.12
  15.9 0.7 copy-start.13
  16.5 0.7 copy-start.14
  17.2 8.6 %copy-start.2 = (bf16[2,1024,512]{2,1,0:T(8,128)(2,1)S(1)}, bf16[2,1024,512]{2,1,0:T(8,128)(2,1)}, u32[]{:S(2)}) copy-start(bf16[2,1024,512]{2,1,0:T(8,128)(2,1)} %wg_hbm.1) | copy-start | bytes 6291460
  17.2 8.7 %copy-start.3 = (bf16[2,1024,512]{2,1,0:T(8,128)(2,1)S(1)}, bf16[2,1024,512]{2,1,0:T(8,128)(2,1)}, u32[]{:S(2)}) copy-start(bf16[2,1024,512]{2,1,0:T(8,128)(2,1)} %wu_hbm.1) | copy-start | bytes 6291460
  17.2 8.7 %copy-start.4 = (bf16[2,512,1024]{2,1,0:T(8,128)(2,1)S(1)}, bf16[2,512,1024]{2,1,0:T(8,128)(2,1)}, u32[]{:S(2)}) copy-start(bf16[2,512,1024]{2,1,0:T(8,128)(2,1)} %wd_hbm.1) | copy-start | bytes 6291460

commit v2 on v1

--- a/solution.py
+++ b/solution.py
@@ -15,10 +15,15 @@
 MESH = pl.DeviceIdType.MESH
 
 
-def attend_kernel(h_ref, lens_ref, ids_ref, ln_a_ref, qg_ref, kg_ref, ln_m_ref, freq_ref, wr_ref,
+def in_hbm(*arrays):
+    return [pltpu.with_memory_space_constraint(a, pltpu.HBM) for a in arrays]
+
+
+def attend_kernel(h_hbm, lens_hbm, ids_hbm, ln_a_hbm, qg_hbm, kg_hbm, ln_m_hbm, wr_hbm,
                   wq_hbm, wk_hbm, wv_hbm, wo_hbm, kc_hbm, vc_hbm,
                   kn_hbm, vn_hbm, y_ref, r_ref, gate_ref,
-                  kbuf, vbuf, wq, wk, wv, wo, qrot, knew, vnew, score, attn, in_sem, out_sem):
+                  h_ref, lens_ref, ids_ref, ln_a_ref, qg_ref, kg_ref, ln_m_ref, wr_ref,
+                  kbuf, vbuf, wq, wk, wv, wo, qrot, knew, vnew, score, attn, small_sem, in_sem, out_sem):
     t_max, n_kv, hd, n_seq = kc_hbm.shape
     n_heads = wq_hbm.shape[1] // hd
     grp = n_heads // n_kv
@@ -32,15 +37,28 @@
     v_in = [pltpu.make_async_copy(vc_hbm.at[pl.ds(c * tc, tc)], vbuf.at[pl.ds(c * tc, tc)], in_sem.at[4 + n_chunk + c]) for c in range(n_chunk)]
     k_out = [pltpu.make_async_copy(kbuf.at[pl.ds(c * tc, tc)], kn_hbm.at[pl.ds(c * tc, tc)], out_sem.at[c]) for c in range(n_chunk)]
     v_out = [pltpu.make_async_copy(vbuf.at[pl.ds(c * tc, tc)], vn_hbm.at[pl.ds(c * tc, tc)], out_sem.at[n_chunk + c]) for c in range(n_chunk)]
-    for copy in w_copies[:3] + k_in + v_in + w_copies[3:]:
+    small = [pltpu.make_async_copy(src, dst, small_sem.at[i]) for i, (src, dst) in enumerate((
+        (h_hbm, h_ref), (lens_hbm, lens_ref), (ids_hbm, ids_ref), (ln_a_hbm, ln_a_ref), (qg_hbm, qg_ref), (kg_hbm, kg_ref), (ln_m_hbm, ln_m_ref), (wr_hbm, wr_ref)))]
+    for copy in small + w_copies[:3] + k_in + v_in + w_copies[3:]:
         copy.start()
+    for copy in small:
+        copy.wait()
+
+    def vector(ref):
+        rows = ref[...].astype(F32)
+        return jnp.concatenate([rows[i:i + 1, :] for i in range(rows.shape[0])], axis=1)
 
     h32 = h_ref[...].astype(F32)
     mean_sq = jnp.mean(h32 * h32, axis=1, keepdims=True)
-    x = (h32 * lax.rsqrt(mean_sq + EPS) * ln_a_ref[...].astype(F32)).astype(BF16)
+    x = (h32 * lax.rsqrt(mean_sq + EPS) * vector(ln_a_ref)).astype(BF16)
 
     lens = lens_ref[...]
-    angles = lens.astype(F32) * freq_ref[...]
+    f_iota = lax.broadcasted_iota(jnp.int32, (half, n_seq), 0)
+    inv_freq = np.power(np.float32(ROPE_BASE), -np.arange(0, hd, 2).astype(np.float32) / np.float32(hd))
+    freq = jnp.zeros((half, n_seq), F32)
+    for i in range(half):
+        freq = jnp.where(f_iota == i, float(inv_freq[i]), freq)
+    angles = lens.astype(F32) * freq
     cos_v = jnp.cos(angles)
     sin_v = jnp.sin(angles)
 
@@ -125,7 +143,7 @@
     y = h32 + jnp.dot(a_rows, wo[...], preferred_element_type=F32)
     y_ref[...] = y
     mean_sq = jnp.mean(y * y, axis=1, keepdims=True)
-    r = (y * lax.rsqrt(mean_sq + EPS) * ln_m_ref[...].astype(F32)).astype(BF16)
+    r = (y * lax.rsqrt(mean_sq + EPS) * vector(ln_m_ref)).astype(BF16)
     r_ref[...] = r
     logits = lax.dot_general(wr_ref[...], r, (((1,), (1,)), ((), ())), preferred_element_type=F32)
     e_iota = lax.broadcasted_iota(jnp.int32, logits.shape, 0)
@@ -147,10 +165,9 @@
     hq, hk = w_q.shape[1], w_k.shape[1]
     n_heads = hq // hd
     n_exp = w_router_t.shape[0]
-    freq = np.power(ROPE_BASE, -np.arange(0, hd, 2).astype(np.float32) / hd).astype(np.float32)
-    freq = jnp.asarray(np.broadcast_to(freq[:, None], (hd // 2, n_seq)))
     vm = pl.BlockSpec(memory_space=pltpu.VMEM)
-    anyspace = pl.BlockSpec(memory_space=pl.ANY)
+    hbm = pl.BlockSpec(memory_space=pltpu.HBM)
+    small = (hidden, lens, ids_t, ln_attn, q_gain, k_gain, ln_moe, w_router_t)
     return pl.pallas_call(
         attend_kernel,
         out_shape=(
@@ -160,18 +177,18 @@
             jax.ShapeDtypeStruct((n_seq, d), BF16),
             jax.ShapeDtypeStruct((n_exp, n_seq), F32),
         ),
-        in_specs=[vm] * 9 + [anyspace] * 6,
-        out_specs=(anyspace, anyspace, vm, vm, vm),
-        scratch_shapes=[
+        in_specs=[hbm] * 14,
+        out_specs=(hbm, hbm, vm, vm, vm),
+        scratch_shapes=[pltpu.VMEM(a.shape, a.dtype) for a in small] + [
             pltpu.VMEM(k_t.shape, BF16), pltpu.VMEM(v_t.shape, BF16),
             pltpu.VMEM(w_q.shape, BF16), pltpu.VMEM(w_k.shape, BF16), pltpu.VMEM(w_v.shape, BF16), pltpu.VMEM(w_o.shape, BF16),
             pltpu.VMEM((hq, n_seq), F32), pltpu.VMEM((hk, n_seq), F32), pltpu.VMEM((hk, n_seq), F32),
             pltpu.VMEM((n_heads, t_max, n_seq), F32), pltpu.VMEM((hq, n_seq), F32),
-            pltpu.SemaphoreType.DMA((12,)), pltpu.SemaphoreType.DMA((8,)),
+            pltpu.SemaphoreType.DMA((len(small),)), pltpu.SemaphoreType.DMA((12,)), pltpu.SemaphoreType.DMA((8,)),
         ],
         compiler_params=pltpu.CompilerParams(vmem_limit_bytes=30 * 1024 * 1024),
         name="attend",
-    )(hidden, lens, ids_t, ln_attn, q_gain, k_gain, ln_moe, freq, w_router_t, w_q, w_k, w_v, w_o, k_t, v_t)
+    )(*in_hbm(*small, w_q, w_k, w_v, w_o, k_t, v_t))
 
 
 def moe_kernel(n, r_ref, gate_ref, y_ref, wg_hbm, wu_hbm, wd_hbm, out_ref,
@@ -432,13 +449,13 @@
     n_exp = gates.shape[0]
     n_local, _, ff = w_gate.shape
     vm = pl.BlockSpec(memory_space=pltpu.VMEM)
-    anyspace = pl.BlockSpec(memory_space=pl.ANY)
+    hbm = pl.BlockSpec(memory_space=pltpu.HBM)
     dma = pltpu.SemaphoreType.DMA
     n_rs = 2 * (n - 1)
     return pl.pallas_call(
         functools.partial(moe_kernel, n),
         out_shape=jax.ShapeDtypeStruct((rows, d), BF16),
-        in_specs=[vm] * 3 + [anyspace] * 3,
+        in_specs=[vm] * 3 + [hbm] * 3,
         out_specs=vm,
         scratch_shapes=[
             pltpu.VMEM((n, 2, rows, d), BF16),
@@ -458,7 +475,7 @@
         ],
         compiler_params=pltpu.CompilerParams(collective_id=0, has_side_effects=True, vmem_limit_bytes=40 * 1024 * 1024),
         name="moe",
-    )(r, gates, y, w_gate, w_up, w_down)
+    )(r, gates, y, *in_hbm(w_gate, w_up, w_down))
 
 
 def solution(mesh):
@@ -474,8 +491,8 @@
         k_t = jnp.transpose(k_cache, (1, 2, 3, 0))
         v_t = jnp.transpose(v_cache, (1, 2, 3, 0))
         k_new, v_new, y, r, gates = attend(
-            hidden, k_t, v_t, seq_lens[None, :], expert_ids.T, ln_attn[None, :], w_q, w_k, w_v,
-            q_gain[None, :], k_gain[None, :], w_o, ln_moe[None, :], w_router.T)
+            hidden, k_t, v_t, seq_lens[None, :], expert_ids.T, ln_attn.reshape(-1, 128), w_q, w_k, w_v,
+            q_gain[None, :], k_gain[None, :], w_o, ln_moe.reshape(-1, 128), w_router.T)
         out = moe(n_ep, r, gates, y, w_gate, w_up, w_down)
         return out, jnp.transpose(k_new, (3, 0, 1, 2)), jnp.transpose(v_new, (3, 0, 1, 2))
 

time: 107 us -> 93.3 us (0.87)
  local copies, waits for them, and re-layouts: 17.3 us -> 0.71 us
  Pallas kernels: 88.1 us -> 91.9 us
    unnamed x31 -> x1, local copies, waits for them, and re-layouts: 15.2 us -> 0.71 us
    pallas_call x1, Pallas kernels: 8.63 us -> 12.4 us  [attend(): pl.pallas_call(attend_kernel, out_shape=(jax.ShapeDtypeStruct(k_t.shape,...]
    broadcast_in_dim x2 -> x0, local copies, waits for them, and re-layouts: 1.37 us -> none  [the longest x1 0.69 us: local_step(): ln_attn[None, :]]
where the time goes in v2:
time: 93.3 us; the launch traced here: 93.2 us
  Pallas kernels  91.9 us (98%)
    pallas_call x1, Pallas kernels, moe(): pl.pallas_call(functools.partial(moe_kernel, n), out_shape=jax.ShapeDtype...  79.5 us
    pallas_call x1, Pallas kernels, attend(): pl.pallas_call(attend_kernel, out_shape=(jax.ShapeDtypeStruct(k_t.shape,...  12.4 us

profile of v2, /device:TPU:21, one launch (start us, length us, event | category | flops | bytes accessed | tf_op | source)
XLA Modules:
  0.0 93.2 jit_solution(17195447494338532565)
XLA Ops:
  0.6 12.4 %attend.1 = (bf16[32,8,64,128]{3,2,1,0:T(8,128)(2,1)}, bf16[32,8,64,128]{3,2,1,0:T(8,128)(2,1)}, f32[128,1024]{1,0:T(8,128)S(1)}, bf16[128,1024]{1,0:T(8,128)(2,1)S(1)}, f32[32,128]{1,0:T(8,128)S(1)}) custom-call(bf16[128,1024]{1,0:T(8,128)(2,1)} %h_hbm.1, s32[1,128]{1,0:T(1,128)} %bitcast.17, s32[8,128]{1,0:T(8,128)} %bitcast.14, bf16[8,128]{1,0:T(8,128)(2,1)} %bitcast.15, ...), custom_call_target="tpu_custom_call" | custom-call | tf_op jit(solution)/shard_map/attend/pallas_call | solution.py:171
  13.1 79.5 %moe.1 = bf16[128,1024]{1,0:T(8,128)(2,1)S(1)} custom-call(bf16[128,1024]{1,0:T(8,128)(2,1)S(1)} %get-tuple-element.8.r_ref, f32[32,128]{1,0:T(8,128)S(1)} %get-tuple-element.9.gate_ref, f32[128,1024]{1,0:T(8,128)S(1)} %get-tuple-element.10.y_ref, bf16[2,1024,512]{2,1,0:T(8,128)(2,1)} %wg_hbm.1, bf16[2,1024,512]{2,1,0:T(8,128)(2,1)} %wu_hbm.1, ...), custom_call_target="tpu_custom_call" | custom-call | tf_op jit(solution)/shard_map/moe/pallas_call | solution.py:455
  92.5 0.7 copy.21

commit v3 on v2

v3 whole, which is shorter than its diff:
```python
import functools

import jax
import jax.numpy as jnp
import numpy as np
from jax import lax
from jax.experimental import pallas as pl
from jax.experimental.pallas import tpu as pltpu
from jax.sharding import PartitionSpec as P

EPS = 1e-6
ROPE_BASE = 1000000.0
F32 = jnp.float32
BF16 = jnp.bfloat16
MESH = pl.DeviceIdType.MESH


def in_hbm(*arrays):
    return [pltpu.with_memory_space_constraint(a, pltpu.HBM) for a in arrays]


def attend_kernel(h_hbm, lens_hbm, ids_hbm, ln_a_hbm, qg_hbm, kg_hbm, ln_m_hbm, wr_hbm,
                  wq_hbm, wk_hbm, wv_hbm, wo_hbm, kc_hbm, vc_hbm,
                  kn_hbm, vn_hbm, y_ref, r_ref, gate_ref,
                  h_ref, lens_ref, ids_ref, ln_a_ref, qg_ref, kg_ref, ln_m_ref, wr_ref,
                  kbuf, vbuf, wq, wk, wv, wo, qrot, knew, vnew, score, attn, small_sem, in_sem, out_sem):
    t_max, n_kv, hd, n_seq = kc_hbm.shape
    n_heads = wq_hbm.shape[1] // hd
    grp = n_heads // n_kv
    half = hd // 2
    n_chunk = 4
    tc = t_max // n_chunk

    w_copies = [pltpu.make_async_copy(src, dst, in_sem.at[i])
                for i, (src, dst) in enumerate(((wk_hbm, wk), (wq_hbm, wq), (wv_hbm, wv), (wo_hbm, wo)))]
    k_in = [pltpu.make_async_copy(kc_hbm.at[pl.ds(c * tc, tc)], kbuf.at[pl.ds(c * tc, tc)], in_sem.at[4 + c]) for c in range(n_chunk)]
    v_in = [pltpu.make_async_copy(vc_hbm.at[pl.ds(c * tc, tc)], vbuf.at[pl.ds(c * tc, tc)], in_sem.at[4 + n_chunk + c]) for c in range(n_chunk)]
    k_out = [pltpu.make_async_copy(kbuf.at[pl.ds(c * tc, tc)], kn_hbm.at[pl.ds(c * tc, tc)], out_sem.at[c]) for c in range(n_chunk)]
    v_out = [pltpu.make_async_copy(vbuf.at[pl.ds(c * tc, tc)], vn_hbm.at[pl.ds(c * tc, tc)], out_sem.at[n_chunk + c]) for c in range(n_chunk)]
    small = [pltpu.make_async_copy(src, dst, small_sem.at[i]) for i, (src, dst) in enumerate((
        (h_hbm, h_ref), (lens_hbm, lens_ref), (ids_hbm, ids_ref), (ln_a_hbm, ln_a_ref), (qg_hbm, qg_ref), (kg_hbm, kg_ref), (ln_m_hbm, ln_m_ref), (wr_hbm, wr_ref)))]
    for copy in small + w_copies[:3]:
        copy.start()
    for copy in small:
        copy.wait()
    k_in[0].start()

    def vector(ref):
        rows = ref[...].astype(F32)
        return jnp.concatenate([rows[i:i + 1, :] for i in range(rows.shape[0])], axis=1)

    h32 = h_ref[...].astype(F32)
    mean_sq = jnp.mean(h32 * h32, axis=1, keepdims=True)
    x = (h32 * lax.rsqrt(mean_sq + EPS) * vector(ln_a_ref)).astype(BF16)

    lens = lens_ref[...]
    f_iota = lax.broadcasted_iota(jnp.int32, (half, n_seq), 0)
    inv_freq = np.power(np.float32(ROPE_BASE), -np.arange(0, hd, 2).astype(np.float32) / np.float32(hd))
    freq = jnp.zeros((half, n_seq), F32)
    for i in range(half):
        freq = jnp.where(f_iota == i, float(inv_freq[i]), freq)
    angles = lens.astype(F32) * freq
    cos_v = jnp.cos(angles)
    sin_v = jnp.sin(angles)

    def gain_tile(g_ref):
        row = g_ref[...].astype(F32)
        row = jnp.concatenate([row] * (n_seq // hd), axis=1)
        return jnp.transpose(jnp.broadcast_to(row, (n_seq, n_seq)))[:hd, :]

    def rope_heads(proj, gain, dst, heads):
        for i in range(heads):
            if i % 2 == 0:
                pair = jnp.transpose(proj[:, i * hd:(i + 2) * hd])
            vals = pair[(i % 2) * hd:(i % 2 + 1) * hd, :]
            ms = jnp.mean(vals * vals, axis=0, keepdims=True)
            vals = vals * lax.rsqrt(ms + EPS) * gain
            low, high = vals[:half, :], vals[half:, :]
            dst[i * hd:i * hd + half, :] = (low * cos_v - high * sin_v).astype(BF16).astype(F32)
            dst[i * hd + half:(i + 1) * hd, :] = (high * cos_v + low * sin_v).astype(BF16).astype(F32)

    w_copies[0].wait()
    for copy in k_in[1:]:
        copy.start()
    rope_heads(jnp.dot(x, wk[...], preferred_element_type=F32), gain_tile(kg_ref), knew, n_kv)
    w_copies[1].wait()
    for copy in v_in + w_copies[3:]:
        copy.start()
    rope_heads(jnp.dot(x, wq[...], preferred_element_type=F32), gain_tile(qg_ref), qrot, n_heads)
    w_copies[2].wait()
    v_proj = jnp.dot(x, wv[...], preferred_element_type=F32)
    for i in range(0, n_kv, 2):
        vnew[i * hd:(i + 2) * hd, :] = jnp.transpose(v_proj[:, i * hd:(i + 2) * hd]).astype(BF16).astype(F32)

    for c in range(n_chunk):
        k_in[c].wait()

        def k_body(kv, carry, c=c):
            new = knew[pl.ds(pl.multiple_of(kv * hd, hd), hd), :]
            qs = [qrot[pl.ds(pl.multiple_of((kv * grp + g) * hd, hd), hd), :] for g in range(grp)]
            rows = [[] for _ in range(grp)]
            for tt in range(tc):
                t = c * tc + tt
                kt = jnp.where(lens == t, new, kbuf[t, kv].astype(F32))
                kbuf[t, kv] = kt.astype(BF16)
                for g in range(grp):
                    rows[g].append(jnp.sum(kt * qs[g], axis=0, keepdims=True))
            for g in range(grp):
                score[kv * grp + g, c * tc:(c + 1) * tc, :] = jnp.concatenate(rows[g], axis=0)
            return carry

        lax.fori_loop(0, n_kv, k_body, 0)
        k_out[c].start()

    visible = lax.broadcasted_iota(jnp.int32, (t_max, n_seq), 0) <= lens

    def soft_body(j, carry):
        s = jnp.where(visible, score[j] * (hd ** -0.5), -1e30)
        e = jnp.exp(s - jnp.max(s, axis=0, keepdims=True))
        score[j] = (e / jnp.sum(e, axis=0, keepdims=True)).astype(BF16).astype(F32)
        return carry

    lax.fori_loop(0, n_heads, soft_body, 0, unroll=2)

    for c in range(n_chunk):
        v_in[c].wait()

        def v_body(kv, carry, c=c):
            new = vnew[pl.ds(pl.multiple_of(kv * hd, hd), hd), :]
            at = [pl.ds(pl.multiple_of((kv * grp + g) * hd, hd), hd) for g in range(grp)]
            acc = [None if c == 0 else attn[at[g], :] for g in range(grp)]
            for tt in range(tc):
                t = c * tc + tt
                vt = jnp.where(lens == t, new, vbuf[t, kv].astype(F32))
                vbuf[t, kv] = vt.astype(BF16)
                for g in range(grp):
                    term = vt * score[kv * grp + g, t:t + 1, :]
                    acc[g] = term if acc[g] is None else acc[g] + term
            for g in range(grp):
                attn[at[g], :] = acc[g]
            return carry

        lax.fori_loop(0, n_kv, v_body, 0)
        v_out[c].start()

    w_copies[3].wait()
    a_rows = jnp.concatenate([jnp.transpose(attn[i * n_seq:(i + 1) * n_seq, :]).astype(BF16) for i in range(n_heads * hd // n_seq)], axis=1)
    y = h32 + jnp.dot(a_rows, wo[...], preferred_element_type=F32)
    y_ref[...] = y
    mean_sq = jnp.mean(y * y, axis=1, keepdims=True)
    r = (y * lax.rsqrt(mean_sq + EPS) * vector(ln_m_ref)).astype(BF16)
    r_ref[...] = r
    logits = lax.dot_general(wr_ref[...], r, (((1,), (1,)), ((), ())), preferred_element_type=F32)
    e_iota = lax.broadcasted_iota(jnp.int32, logits.shape, 0)
    ids = ids_ref[...]
    chosen = e_iota == ids[0:1, :]
    for i in range(1, ids.shape[0]):
        chosen = chosen | (e_iota == ids[i:i + 1, :])
    top = jnp.max(jnp.where(chosen, logits, -jnp.inf), axis=0, keepdims=True)
    e = jnp.where(chosen, jnp.exp(logits - top), 0.0)
    gates = jnp.where(chosen, e / jnp.sum(e, axis=0, keepdims=True), -1.0)
    g_rows = gates.shape[0] // 2
    turned = pltpu.roll(gates, n_seq // 2, 1)
    low = lax.broadcasted_iota(jnp.int32, (g_rows, n_seq), 1) < n_seq // 2
    gate_ref[0] = jnp.where(low, gates[:g_rows, :], turned[g_rows:, :])
    gate_ref[1] = jnp.where(low, turned[:g_rows, :], gates[g_rows:, :])

    for copy in k_out + v_out:
        copy.wait()


def attend(hidden, k_t, v_t, lens, ids_t, ln_attn, w_q, w_k, w_v, q_gain, k_gain, w_o, ln_moe, w_router_t):
    n_seq, d = hidden.shape
    t_max, n_kv, hd, _ = k_t.shape
    hq, hk = w_q.shape[1], w_k.shape[1]
    n_heads = hq // hd
    n_exp = w_router_t.shape[0]
    vm = pl.BlockSpec(memory_space=pltpu.VMEM)
    hbm = pl.BlockSpec(memory_space=pltpu.HBM)
    small = (hidden, lens, ids_t, ln_attn, q_gain, k_gain, ln_moe, w_router_t)
    return pl.pallas_call(
        attend_kernel,
        out_shape=(
            jax.ShapeDtypeStruct(k_t.shape, k_t.dtype),
            jax.ShapeDtypeStruct(v_t.shape, v_t.dtype),
            jax.ShapeDtypeStruct((n_seq, d), F32),
            jax.ShapeDtypeStruct((n_seq, d), BF16),
            jax.ShapeDtypeStruct((2, n_exp // 2, n_seq), F32),
        ),
        in_specs=[hbm] * 14,
        out_specs=(hbm, hbm, vm, vm, vm),
        scratch_shapes=[pltpu.VMEM(a.shape, a.dtype) for a in small] + [
            pltpu.VMEM(k_t.shape, BF16), pltpu.VMEM(v_t.shape, BF16),
            pltpu.VMEM(w_q.shape, BF16), pltpu.VMEM(w_k.shape, BF16), pltpu.VMEM(w_v.shape, BF16), pltpu.VMEM(w_o.shape, BF16),
            pltpu.VMEM((hq, n_seq), F32), pltpu.VMEM((hk, n_seq), F32), pltpu.VMEM((hk, n_seq), F32),
            pltpu.VMEM((n_heads, t_max, n_seq), F32), pltpu.VMEM((hq, n_seq), F32),
            pltpu.SemaphoreType.DMA((len(small),)), pltpu.SemaphoreType.DMA((12,)), pltpu.SemaphoreType.DMA((8,)),
        ],
        compiler_params=pltpu.CompilerParams(vmem_limit_bytes=30 * 1024 * 1024),
        name="attend",
    )(*in_hbm(*small, w_q, w_k, w_v, w_o, k_t, v_t))


def rs_order(half):
    seq = [(half - 1, 0, 0), (half - 1, 0, 1)]
    for q in range(half, 3, -1):
        seq += [(q - 2, 0, 0), (q, 1, 0), (q, 1, 1), (q - 2, 0, 1)]
    return seq + [(3, 1, 0), (3, 1, 1), (1, 0, 0), (2, 1, 0), (2, 1, 1), (1, 0, 1), (1, 1, 0), (1, 1, 1)]


def moe_kernel(n, r_ref, gate_ref, y_ref, wg_hbm, wu_hbm, wd_hbm, out_ref,
               xbuf, gbuf, cbuf, cpart, inc, wg, wu, wd, act, gcol,
               w_sem, ring_send, ring_recv, gate_send, gate_recv,
               pair_send, pair_recv, pgate_send, pgate_recv,
               sum_send, sum_recv, rs_send, rs_recv):
    me = lax.axis_index("ep")
    chip = me // 2
    core = lax.rem(me, 2)
    other = 1 - core
    half = n // 2
    rows, d = r_ref.shape
    n_local = wg_hbm.shape[0]
    g_rows = gate_ref.shape[1]
    hr = rows // 2
    qr = hr // 2
    ring = [{"ep": 2 * lax.rem(chip + 1, n) + core}, {"ep": 2 * lax.rem(chip + n - 1, n) + core}]
    pair = {"ep": 2 * chip + other}

    def remote(src, dst, ssem, rsem, dev):
        return pltpu.make_async_remote_copy(src_ref=src, dst_ref=dst, send_sem=ssem, recv_sem=rsem, device_id=dev, device_id_type=MESH)

    barrier = pltpu.get_barrier_semaphore()
    for dev in ring + [pair]:
        pl.semaphore_signal(barrier, inc=1, device_id=dev, device_id_type=MESH)
    w_copies = [pltpu.make_async_copy(src, dst, w_sem.at[i]) for i, (src, dst) in enumerate(((wg_hbm, wg), (wu_hbm, wu), (wd_hbm, wd)))]
    for copy in w_copies:
        copy.start()
    pl.semaphore_wait(barrier, 3)

    def ring_copies(direction, v, x_src, g_src):
        return [remote(g_src, gbuf.at[v + 1, direction, core], gate_send.at[direction, v], gate_recv.at[direction, v], ring[direction]),
                remote(x_src, xbuf.at[v + 1, direction, core], ring_send.at[direction, v], ring_recv.at[direction, v], ring[direction])]

    def pair_copies(direction, k, c, x_src, g_src):
        return [remote(g_src, gbuf.at[k, direction, c], pgate_send.at[k, direction], pgate_recv.at[k, direction], pair),
                remote(x_src, xbuf.at[k, direction, c], pair_send.at[k, direction], pair_recv.at[k, direction], pair)]

    def held(direction, k, c):
        return xbuf.at[k, direction, c], gbuf.at[k, direction, c]

    def own(h):
        return r_ref.at[pl.ds(h * hr, hr)], gate_ref.at[h]

    def own_half(direction, v):
        return v if direction == 0 else 1 - v

    for v in range(2):
        for direction in range(2):
            for copy in ring_copies(direction, v, *own(own_half(direction, v))):
                copy.start()
        if v == 0:
            for h in range(2):
                for copy in pair_copies(h, 0, core, *own(h)):
                    copy.start()
    for h in range(2):
        xbuf[0, h, core] = r_ref[h * hr:(h + 1) * hr, :]
        gbuf[0, h, core] = gate_ref[h]

    def sum_copy(k, direction):
        return remote(cbuf.at[k, direction, other], cpart.at[k, direction], sum_send.at[k, direction], sum_recv.at[k, direction], pair)

    order = rs_order(half)

    def rs_place(direction, u):
        q, long_half, p = order[u]
        if long_half and q == half:
            return 2 * q - 1, direction, pl.ds(p * qr, qr)
        return 2 * q - 1 + long_half, 1 - direction, pl.ds(p * qr, qr)

    def rs_copy(direction, u):
        q, long_half, p = order[u]
        k, side, at = rs_place(direction, u)
        return remote(cbuf.at[k, side, core, at], inc.at[direction, q - 1, long_half, at], rs_send.at[direction, u], rs_recv.at[direction, u], ring[direction])

    def rs_step(direction, u):
        q, long_half, p = order[u]
        k, side, at = rs_place(direction, u)
        total = cbuf[k, side, core, at, :] + cpart[k, side, at, :]
        if (q + 1, long_half, p) in order:
            rs_copy(direction, order.index((q + 1, long_half, p))).wait_recv()
            total = total + inc[direction, q, long_half, at, :]
        cbuf[k, side, core, at, :] = total
        rs_copy(direction, u).start()

    e_first = n_local * me
    e_side = e_first // g_rows
    e_row = e_first - e_side * g_rows
    low_lanes = lax.broadcasted_iota(jnp.int32, (1, rows), 1) < hr

    def compute(k):
        x = xbuf[k].reshape(2 * rows, d)
        for e in range(n_local):
            for direction in range(2):
                a, b = [gbuf[k, direction, c, pl.ds(e_row + e, 1), :] for c in range(2)]
                ra, rb = pltpu.roll(a, hr, 1), pltpu.roll(b, hr, 1)
                row = jnp.where(low_lanes, jnp.where(e_side == 0, a, ra), jnp.where(e_side == 0, rb, b))
                gcol[e, direction * rows:(direction + 1) * rows, :] = jnp.transpose(jnp.broadcast_to(row, (rows, rows)))
        ft = 256
        for e in range(n_local):
            for nt in range(wg.shape[2] // ft):
                cols = slice(nt * ft, (nt + 1) * ft)
                g = jnp.dot(x, wg[e, :, cols], preferred_element_type=F32)
                u = jnp.dot(x, wu[e, :, cols], preferred_element_type=F32)
                act[:, cols] = (jax.nn.silu(g) * u).astype(BF16)
            a = act[...]
            gc = gcol[e]
            chosen = gc >= 0.0
            for nt in range(d // ft):
                f = jnp.dot(a, wd[e, :, nt * ft:(nt + 1) * ft], preferred_element_type=F32).astype(BF16).astype(F32)
                for l in range(ft // rows):
                    cols = slice(nt * ft + l * rows, nt * ft + (l + 1) * rows)
                    term = jnp.where(chosen, f[:, l * rows:(l + 1) * rows] * gc, 0.0).reshape(2, 2, hr, rows)
                    cbuf[k, :, :, :, cols] = term if e == 0 else cbuf[k, :, :, :, cols] + term

    for copy in w_copies:
        copy.wait()

    def body(k, carry):
        @pl.when(k > 0)
        def _():
            for direction in range(2):
                x_src, g_src = held(direction, k, core)
                for copy in ring_copies(direction, k - 1, x_src, g_src):
                    copy.wait_recv()

                @pl.when(k <= n - 3)
                def _():
                    for copy in ring_copies(direction, k + 1, x_src, g_src):
                        copy.start()

                for copy in pair_copies(direction, k, core, x_src, g_src):
                    copy.start()

        for direction in range(2):
            for copy in pair_copies(direction, k, other, *held(direction, k, other)):
                copy.wait_recv()

        @pl.when(k == n - 2)
        def _():
            for side in range(2):
                sum_copy(n - 3, side).wait_recv()
            for u in range(2):
                for direction in range(2):
                    rs_step(direction, u)

        compute(k)
        for direction in range(2):
            sum_copy(k, direction).start()
        return carry

    lax.fori_loop(0, n, body, 0)

    summed = {(n - 3, 0), (n - 3, 1)}

    def wait_sum(k, side):
        if (k, side) not in summed:
            sum_copy(k, side).wait_recv()
            summed.add((k, side))

    for u in range(2, len(order)):
        for direction in range(2):
            wait_sum(*rs_place(direction, u)[:2])
            rs_step(direction, u)
    for h in range(2):
        wait_sum(0, h)
    for long_half, p in ((0, 0), (0, 1), (1, 0), (1, 1)):
        u = order.index((1, long_half, p))
        for direction in range(2):
            h = 1 - long_half if direction == 0 else long_half
            rs_copy(direction, u).wait_recv()
            at = pl.ds(h * hr + p * qr, qr)
            part = pl.ds(p * qr, qr)
            got = inc[direction, 0, long_half, part, :]
            if long_half == 0:
                cbuf[0, h, core, part, :] = y_ref[at, :] + ((cbuf[0, h, core, part, :] + cpart[0, h, part, :]) + got)
            else:
                out_ref[at, :] = (cbuf[0, h, core, part, :] + got).astype(out_ref.dtype)

    for direction in range(2):
        for v in range(n - 1):
            src = own(own_half(direction, v)) if v < 2 else held(direction, v - 1, core)
            for copy in ring_copies(direction, v, *src):
                copy.wait_send()
        for k in range(n):
            src = own(direction) if k == 0 else held(direction, k, core)
            for copy in pair_copies(direction, k, core, *src):
                copy.wait_send()
            sum_copy(k, direction).wait_send()
        for u in range(len(order)):
            rs_copy(direction, u).wait_send()


def moe(n_ep, r, gates, y, w_gate, w_up, w_down):
    n = n_ep // 2
    rows, d = r.shape
    n_local, _, ff = w_gate.shape
    vm = pl.BlockSpec(memory_space=pltpu.VMEM)
    hbm = pl.BlockSpec(memory_space=pltpu.HBM)
    dma = pltpu.SemaphoreType.DMA
    n_rs = 2 * (n - 1)
    return pl.pallas_call(
        functools.partial(moe_kernel, n),
        out_shape=jax.ShapeDtypeStruct((rows, d), BF16),
        in_specs=[vm] * 3 + [hbm] * 3,
        out_specs=vm,
        scratch_shapes=[
            pltpu.VMEM((n, 2, 2, rows // 2, d), BF16),
            pltpu.VMEM((n, 2, 2) + gates.shape[1:], F32),
            pltpu.VMEM((n, 2, 2, rows // 2, d), F32),
            pltpu.VMEM((n, 2, rows // 2, d), F32),
            pltpu.VMEM((2, n // 2, 2, rows // 2, d), F32),
            pltpu.VMEM(w_gate.shape, BF16), pltpu.VMEM(w_up.shape, BF16), pltpu.VMEM(w_down.shape, BF16),
            pltpu.VMEM((2 * rows, ff), BF16),
            pltpu.VMEM((n_local, 2 * rows, rows), F32),
            dma((3,)),
            dma((2, n - 1)), dma((2, n - 1)), dma((2, n - 1)), dma((2, n - 1)),
            dma((n, 2)), dma((n, 2)), dma((n, 2)), dma((n, 2)),
            dma((n, 2)), dma((n, 2)),
            dma((2, n_rs)), dma((2, n_rs)),
        ],
        compiler_params=pltpu.CompilerParams(collective_id=0, has_side_effects=True, vmem_limit_bytes=40 * 1024 * 1024),
        name="moe",
    )(r, gates, y, *in_hbm(w_gate, w_up, w_down))


def solution(mesh):
    n_ep = mesh.shape['ep']
    row_spec = P(('dp', 'ep'), None)
    cache_spec = P(('dp', 'ep'), None, None, None)
    len_spec = P(('dp', 'ep'))
    rep_vec = P(None)
    rep_mat = P(None, None)
    exp_spec = P('ep', None, None)

    def local_step(hidden, k_cache, v_cache, seq_lens, expert_ids, ln_attn, w_q, w_k, w_v, q_gain, k_gain, w_o, ln_moe, w_router, w_gate, w_up, w_down):
        k_t = jnp.transpose(k_cache, (1, 2, 3, 0))
        v_t = jnp.transpose(v_cache, (1, 2, 3, 0))
        k_new, v_new, y, r, gates = attend(
            hidden, k_t, v_t, seq_lens[None, :], expert_ids.T, ln_attn.reshape(-1, 128), w_q, w_k, w_v,
            q_gain[None, :], k_gain[None, :], w_o, ln_moe.reshape(-1, 128), w_router.T)
        out = moe(n_ep, r, gates, y, w_gate, w_up, w_down)
        return out, jnp.transpose(k_new, (3, 0, 1, 2)), jnp.transpose(v_new, (3, 0, 1, 2))

    return jax.shard_map(local_step, mesh=mesh, in_specs=(row_spec, cache_spec, cache_spec, len_spec, row_spec, rep_vec, rep_mat, rep_mat, rep_mat, rep_vec, rep_vec, rep_mat, rep_vec, rep_mat, exp_spec, exp_spec, exp_spec), out_specs=(row_spec, cache_spec, cache_spec), check_vma=False)
```

time: 93.3 us -> 89.8 us (0.962)
  Pallas kernels: 91.9 us -> 88.4 us
    pallas_call x1, Pallas kernels: 12.4 us -> 9.76 us  [attend(): pl.pallas_call(attend_kernel, out_shape=(jax.ShapeDtypeStruct(k_t.shape,...]
where the time goes in v3:
time: 89.8 us
  Pallas kernels  88.4 us (98%)
    pallas_call x1, Pallas kernels, moe(): pl.pallas_call(functools.partial(moe_kernel, n), out_shape=jax.ShapeDtype...  78.7 us
    pallas_call x1, Pallas kernels, attend(): pl.pallas_call(attend_kernel, out_shape=(jax.ShapeDtypeStruct(k_t.shape,...  9.76 us

profile of v3, /device:TPU:21, one launch (start us, length us, event | category | flops | bytes accessed | tf_op | source)
XLA Modules:
  0.0 89.8 jit_solution(3447034473165931116)
XLA Ops:
  0.6 9.8 %attend.1 = (bf16[32,8,64,128]{3,2,1,0:T(8,128)(2,1)}, bf16[32,8,64,128]{3,2,1,0:T(8,128)(2,1)}, f32[128,1024]{1,0:T(8,128)S(1)}, bf16[128,1024]{1,0:T(8,128)(2,1)S(1)}, f32[2,16,128]{2,1,0:T(8,128)S(1)}) custom-call(bf16[128,1024]{1,0:T(8,128)(2,1)} %h_hbm.1, s32[1,128]{1,0:T(1,128)} %bitcast.17, s32[8,128]{1,0:T(8,128)} %bitcast.14, ...), custom_call_target="tpu_custom_call" | custom-call | tf_op jit(solution)/shard_map/attend/pallas_call | solution.py:181
  10.4 78.7 %moe.1 = bf16[128,1024]{1,0:T(8,128)(2,1)S(1)} custom-call(bf16[128,1024]{1,0:T(8,128)(2,1)S(1)} %get-tuple-element.8.r_ref, f32[2,16,128]{2,1,0:T(8,128)S(1)} %get-tuple-element.9.gate_ref, f32[128,1024]{1,0:T(8,128)S(1)} %get-tuple-element.10.y_ref, bf16[2,1024,512]{2,1,0:T(8,128)(2,1)} %wg_hbm.1, bf16[2,1024,512]{2,1,0:T(8,128)(2,1)} %wu_hbm.1, ...), custom_call_target="tpu_custom_call" | custom-call | tf_op jit(solution)/shard_map/moe/pallas_call | solution.py:411
  89.1 0.7 copy.21

commit v4 on v3

--- a/solution.py
+++ b/solution.py
@@ -322,28 +322,28 @@
                     term = jnp.where(chosen, f[:, l * rows:(l + 1) * rows] * gc, 0.0).reshape(2, 2, hr, rows)
                     cbuf[k, :, :, :, cols] = term if e == 0 else cbuf[k, :, :, :, cols] + term
 
-    for copy in w_copies:
-        copy.wait()
+    def take(k):
+        for direction in range(2):
+            x_src, g_src = held(direction, k, core)
+            for copy in ring_copies(direction, k - 1, x_src, g_src):
+                copy.wait_recv()
+
+            @pl.when(k <= n - 3)
+            def _():
+                for copy in ring_copies(direction, k + 1, x_src, g_src):
+                    copy.start()
+
+            for copy in pair_copies(direction, k, core, x_src, g_src):
+                copy.start()
 
     def body(k, carry):
-        @pl.when(k > 0)
+        @pl.when(k <= n - 4)
         def _():
-            for direction in range(2):
-                x_src, g_src = held(direction, k, core)
-                for copy in ring_copies(direction, k - 1, x_src, g_src):
-                    copy.wait_recv()
-
-                @pl.when(k <= n - 3)
-                def _():
-                    for copy in ring_copies(direction, k + 1, x_src, g_src):
-                        copy.start()
-
-                for copy in pair_copies(direction, k, core, x_src, g_src):
-                    copy.start()
-
-        for direction in range(2):
-            for copy in pair_copies(direction, k, other, *held(direction, k, other)):
-                copy.wait_recv()
+            take(k + 1)
+
+        @pl.when(k >= n - 2)
+        def _():
+            take(k)
 
         @pl.when(k == n - 2)
         def _():
@@ -353,6 +353,14 @@
                 for direction in range(2):
                     rs_step(direction, u)
 
+        @pl.when(k == 0)
+        def _():
+            for copy in w_copies:
+                copy.wait()
+
+        for direction in range(2):
+            for copy in pair_copies(direction, k, other, *held(direction, k, other)):
+                copy.wait_recv()
         compute(k)
         for direction in range(2):
             sum_copy(k, direction).start()

time: 89.8 us -> 86.1 us (0.959)
  Pallas kernels: 88.4 us -> 84.7 us
    pallas_call x1, Pallas kernels: 78.7 us -> 74.9 us  [moe(): pl.pallas_call(functools.partial(moe_kernel, n), out_shape=jax.ShapeDtype...]
where the time goes in v4:
time: 86.1 us
  Pallas kernels  84.7 us (98%)
    pallas_call x1, Pallas kernels, moe(): pl.pallas_call(functools.partial(moe_kernel, n), out_shape=jax.ShapeDtype...  74.9 us
    pallas_call x1, Pallas kernels, attend(): pl.pallas_call(attend_kernel, out_shape=(jax.ShapeDtypeStruct(k_t.shape,...  9.76 us

profile of v4, /device:TPU:21, one launch (start us, length us, event | category | flops | bytes accessed | tf_op | source)
XLA Modules:
  0.0 86.1 jit_solution(11621105958001776618)
XLA Ops:
  0.6 9.8 %attend.1 = (bf16[32,8,64,128]{3,2,1,0:T(8,128)(2,1)}, bf16[32,8,64,128]{3,2,1,0:T(8,128)(2,1)}, f32[128,1024]{1,0:T(8,128)S(1)}, bf16[128,1024]{1,0:T(8,128)(2,1)S(1)}, f32[2,16,128]{2,1,0:T(8,128)S(1)}) custom-call(bf16[128,1024]{1,0:T(8,128)(2,1)} %h_hbm.1, s32[1,128]{1,0:T(1,128)} %bitcast.17, s32[8,128]{1,0:T(8,128)} %bitcast.14, ...), custom_call_target="tpu_custom_call" | custom-call | tf_op jit(solution)/shard_map/attend/pallas_call | solution.py:181
  10.4 74.9 %moe.1 = bf16[128,1024]{1,0:T(8,128)(2,1)S(1)} custom-call(bf16[128,1024]{1,0:T(8,128)(2,1)S(1)} %get-tuple-element.8.r_ref, f32[2,16,128]{2,1,0:T(8,128)S(1)} %get-tuple-element.9.gate_ref, f32[128,1024]{1,0:T(8,128)S(1)} %get-tuple-element.10.y_ref, bf16[2,1024,512]{2,1,0:T(8,128)(2,1)} %wg_hbm.1, bf16[2,1024,512]{2,1,0:T(8,128)(2,1)} %wu_hbm.1, ...), custom_call_target="tpu_custom_call" | custom-call | tf_op jit(solution)/shard_map/moe/pallas_call | solution.py:419
  85.3 0.7 copy.21

commit v5 on v4

--- a/solution.py
+++ b/solution.py
@@ -202,10 +202,12 @@
 
 
 def rs_order(half):
-    seq = [(half - 1, 0, 0), (half - 1, 0, 1)]
-    for q in range(half, 3, -1):
-        seq += [(q - 2, 0, 0), (q, 1, 0), (q, 1, 1), (q - 2, 0, 1)]
-    return seq + [(3, 1, 0), (3, 1, 1), (1, 0, 0), (2, 1, 0), (2, 1, 1), (1, 0, 1), (1, 1, 0), (1, 1, 1)]
+    seq = [(half - 2, 3), (half - 1, 2), (half + 1, 0), (half, 1)]
+    last = dict((c, q) for q, c in seq)
+    for c in (3, 2, 0, 1, 2, 0, 1, 0, 1, 0):
+        last[c] -= 1
+        seq.append((last[c], c))
+    return seq
 
 
 def moe_kernel(n, r_ref, gate_ref, y_ref, wg_hbm, wu_hbm, wd_hbm, out_ref,
@@ -271,24 +273,35 @@
 
     order = rs_order(half)
 
+    def quarter(direction, chain):
+        return chain if direction == 0 else 3 - chain
+
     def rs_place(direction, u):
-        q, long_half, p = order[u]
-        if long_half and q == half:
-            return 2 * q - 1, direction, pl.ds(p * qr, qr)
-        return 2 * q - 1 + long_half, 1 - direction, pl.ds(p * qr, qr)
+        q, chain = order[u]
+        i = quarter(direction, chain)
+        step = q if direction == 0 else -q
+        step = step - n if step > half else step + n if step <= -half else step
+        h = i // 2
+        if step == half:
+            k, side = n - 1, h
+        elif step > 0:
+            k, side = 2 * step - h, 1
+        else:
+            k, side = -2 * step - 1 + h, 0
+        return k, side, pl.ds((i % 2) * qr, qr)
 
     def rs_copy(direction, u):
-        q, long_half, p = order[u]
+        q, chain = order[u]
         k, side, at = rs_place(direction, u)
-        return remote(cbuf.at[k, side, core, at], inc.at[direction, q - 1, long_half, at], rs_send.at[direction, u], rs_recv.at[direction, u], ring[direction])
+        return remote(cbuf.at[k, side, core, at], inc.at[direction, q - 1, chain], rs_send.at[direction, u], rs_recv.at[direction, u], ring[direction])
 
     def rs_step(direction, u):
-        q, long_half, p = order[u]
+        q, chain = order[u]
         k, side, at = rs_place(direction, u)
         total = cbuf[k, side, core, at, :] + cpart[k, side, at, :]
-        if (q + 1, long_half, p) in order:
-            rs_copy(direction, order.index((q + 1, long_half, p))).wait_recv()
-            total = total + inc[direction, q, long_half, at, :]
+        if (q + 1, chain) in order:
+            rs_copy(direction, order.index((q + 1, chain))).wait_recv()
+            total = total + inc[direction, q, chain]
         cbuf[k, side, core, at, :] = total
         rs_copy(direction, u).start()
 
@@ -345,11 +358,18 @@
         def _():
             take(k)
 
+        @pl.when(k == n - 3)
+        def _():
+            for side in range(2):
+                sum_copy(n - 5, side).wait_recv()
+            for direction in range(2):
+                rs_step(direction, 0)
+
         @pl.when(k == n - 2)
         def _():
             for side in range(2):
                 sum_copy(n - 3, side).wait_recv()
-            for u in range(2):
+            for u in range(1, 3):
                 for direction in range(2):
                     rs_step(direction, u)
 
@@ -368,31 +388,31 @@
 
     lax.fori_loop(0, n, body, 0)
 
-    summed = {(n - 3, 0), (n - 3, 1)}
+    summed = {(n - 5, 0), (n - 5, 1), (n - 3, 0), (n - 3, 1)}
 
     def wait_sum(k, side):
         if (k, side) not in summed:
             sum_copy(k, side).wait_recv()
             summed.add((k, side))
 
-    for u in range(2, len(order)):
+    for u in range(3, len(order)):
         for direction in range(2):
             wait_sum(*rs_place(direction, u)[:2])
             rs_step(direction, u)
     for h in range(2):
         wait_sum(0, h)
-    for long_half, p in ((0, 0), (0, 1), (1, 0), (1, 1)):
-        u = order.index((1, long_half, p))
-        for direction in range(2):
-            h = 1 - long_half if direction == 0 else long_half
+    seen = set()
+    for u, (q, chain) in enumerate(order):
+        for direction in range(2) if q == 1 else ():
             rs_copy(direction, u).wait_recv()
-            at = pl.ds(h * hr + p * qr, qr)
-            part = pl.ds(p * qr, qr)
-            got = inc[direction, 0, long_half, part, :]
-            if long_half == 0:
-                cbuf[0, h, core, part, :] = y_ref[at, :] + ((cbuf[0, h, core, part, :] + cpart[0, h, part, :]) + got)
+            i = quarter(direction, chain)
+            part = pl.ds((i % 2) * qr, qr)
+            at = pl.ds(i * qr, qr)
+            if i in seen:
+                out_ref[at, :] = (cbuf[0, i // 2, core, part, :] + inc[direction, 0, chain]).astype(out_ref.dtype)
             else:
-                out_ref[at, :] = (cbuf[0, h, core, part, :] + got).astype(out_ref.dtype)
+                seen.add(i)
+                cbuf[0, i // 2, core, part, :] = y_ref[at, :] + ((cbuf[0, i // 2, core, part, :] + cpart[0, i // 2, part, :]) + inc[direction, 0, chain])
 
     for direction in range(2):
         for v in range(n - 1):
@@ -426,7 +446,7 @@
             pltpu.VMEM((n, 2, 2) + gates.shape[1:], F32),
             pltpu.VMEM((n, 2, 2, rows // 2, d), F32),
             pltpu.VMEM((n, 2, rows // 2, d), F32),
-            pltpu.VMEM((2, n // 2, 2, rows // 2, d), F32),
+            pltpu.VMEM((2, n // 2 + 1, 4, rows // 4, d), F32),
             pltpu.VMEM(w_gate.shape, BF16), pltpu.VMEM(w_up.shape, BF16), pltpu.VMEM(w_down.shape, BF16),
             pltpu.VMEM((2 * rows, ff), BF16),
             pltpu.VMEM((n_local, 2 * rows, rows), F32),

time: 86.1 us -> 85.5 us (level)
  no operation moved by 1% of the time
where the time goes in v5:
time: 85.5 us; the launch traced here: 85.4 us
  Pallas kernels  84.1 us (98%)
    pallas_call x1, Pallas kernels, moe(): pl.pallas_call(functools.partial(moe_kernel, n), out_shape=jax.ShapeDtype...  74.3 us
    pallas_call x1, Pallas kernels, attend(): pl.pallas_call(attend_kernel, out_shape=(jax.ShapeDtypeStruct(k_t.shape,...  9.76 us

profile of v5, /device:TPU:21, one launch (start us, length us, event | category | flops | bytes accessed | tf_op | source)
XLA Modules:
  0.0 85.4 jit_solution(10252437101680032537)
XLA Ops:
  0.6 9.8 %attend.1 = (bf16[32,8,64,128]{3,2,1,0:T(8,128)(2,1)}, bf16[32,8,64,128]{3,2,1,0:T(8,128)(2,1)}, f32[128,1024]{1,0:T(8,128)S(1)}, bf16[128,1024]{1,0:T(8,128)(2,1)S(1)}, f32[2,16,128]{2,1,0:T(8,128)S(1)}) custom-call(bf16[128,1024]{1,0:T(8,128)(2,1)} %h_hbm.1, s32[1,128]{1,0:T(1,128)} %bitcast.17, s32[8,128]{1,0:T(8,128)} %bitcast.14, ...), custom_call_target="tpu_custom_call" | custom-call | tf_op jit(solution)/shard_map/attend/pallas_call | solution.py:181
  10.4 74.3 %moe.1 = bf16[128,1024]{1,0:T(8,128)(2,1)S(1)} custom-call(bf16[128,1024]{1,0:T(8,128)(2,1)S(1)} %get-tuple-element.8.r_ref, f32[2,16,128]{2,1,0:T(8,128)S(1)} %get-tuple-element.9.gate_ref, f32[128,1024]{1,0:T(8,128)S(1)} %get-tuple-element.10.y_ref, bf16[2,1024,512]{2,1,0:T(8,128)(2,1)} %wg_hbm.1, bf16[2,1024,512]{2,1,0:T(8,128)(2,1)} %wu_hbm.1, ...), custom_call_target="tpu_custom_call" | custom-call | tf_op jit(solution)/shard_map/moe/pallas_call | solution.py:439
  84.7 0.7 copy.21

commit v6 on v5

--- a/solution.py
+++ b/solution.py
@@ -39,7 +39,7 @@
     v_out = [pltpu.make_async_copy(vbuf.at[pl.ds(c * tc, tc)], vn_hbm.at[pl.ds(c * tc, tc)], out_sem.at[n_chunk + c]) for c in range(n_chunk)]
     small = [pltpu.make_async_copy(src, dst, small_sem.at[i]) for i, (src, dst) in enumerate((
         (h_hbm, h_ref), (lens_hbm, lens_ref), (ids_hbm, ids_ref), (ln_a_hbm, ln_a_ref), (qg_hbm, qg_ref), (kg_hbm, kg_ref), (ln_m_hbm, ln_m_ref), (wr_hbm, wr_ref)))]
-    for copy in small + w_copies[:3]:
+    for copy in small + w_copies[:2]:
         copy.start()
     for copy in small:
         copy.wait()
@@ -80,17 +80,23 @@
             dst[i * hd + half:(i + 1) * hd, :] = (high * cos_v + low * sin_v).astype(BF16).astype(F32)
 
     w_copies[0].wait()
-    for copy in k_in[1:]:
+    for copy in k_in[1:] + w_copies[2:3]:
         copy.start()
     rope_heads(jnp.dot(x, wk[...], preferred_element_type=F32), gain_tile(kg_ref), knew, n_kv)
     w_copies[1].wait()
     for copy in v_in + w_copies[3:]:
         copy.start()
     rope_heads(jnp.dot(x, wq[...], preferred_element_type=F32), gain_tile(qg_ref), qrot, n_heads)
-    w_copies[2].wait()
-    v_proj = jnp.dot(x, wv[...], preferred_element_type=F32)
-    for i in range(0, n_kv, 2):
-        vnew[i * hd:(i + 2) * hd, :] = jnp.transpose(v_proj[:, i * hd:(i + 2) * hd]).astype(BF16).astype(F32)
+    sub = lax.broadcasted_iota(jnp.int32, (8, n_seq), 0)
+
+    def fold(terms):
+        top = sub < 4
+        pairs = [jnp.where(top, a, b) + pltpu.roll(jnp.where(top, b, a), 4, 0)
+                 for a, b in ((terms[0], terms[4]), (terms[2], terms[6]), (terms[1], terms[5]), (terms[3], terms[7]))]
+        for shift, keep in ((2, sub % 4 < 2), (1, sub % 2 < 1)):
+            pairs = [jnp.where(keep, a, pltpu.roll(b, shift, 0)) + jnp.where(keep, pltpu.roll(a, 8 - shift, 0), b)
+                     for a, b in zip(pairs[0::2], pairs[1::2])]
+        return pairs[0]
 
     for c in range(n_chunk):
         k_in[c].wait()
@@ -104,13 +110,18 @@
                 kt = jnp.where(lens == t, new, kbuf[t, kv].astype(F32))
                 kbuf[t, kv] = kt.astype(BF16)
                 for g in range(grp):
-                    rows[g].append(jnp.sum(kt * qs[g], axis=0, keepdims=True))
+                    rows[g].append(jnp.sum((kt * qs[g]).reshape(hd // 8, 8, n_seq), axis=0))
             for g in range(grp):
-                score[kv * grp + g, c * tc:(c + 1) * tc, :] = jnp.concatenate(rows[g], axis=0)
+                score[kv * grp + g, c * tc:(c + 1) * tc, :] = fold(rows[g])
             return carry
 
         lax.fori_loop(0, n_kv, k_body, 0)
         k_out[c].start()
+
+    w_copies[2].wait()
+    v_proj = jnp.dot(x, wv[...], preferred_element_type=F32)
+    for i in range(0, n_kv, 2):
+        vnew[i * hd:(i + 2) * hd, :] = jnp.transpose(v_proj[:, i * hd:(i + 2) * hd]).astype(BF16).astype(F32)
 
     visible = lax.broadcasted_iota(jnp.int32, (t_max, n_seq), 0) <= lens
 
@@ -158,12 +169,12 @@
         chosen = chosen | (e_iota == ids[i:i + 1, :])
     top = jnp.max(jnp.where(chosen, logits, -jnp.inf), axis=0, keepdims=True)
     e = jnp.where(chosen, jnp.exp(logits - top), 0.0)
-    gates = jnp.where(chosen, e / jnp.sum(e, axis=0, keepdims=True), -1.0)
-    g_rows = gates.shape[0] // 2
-    turned = pltpu.roll(gates, n_seq // 2, 1)
-    low = lax.broadcasted_iota(jnp.int32, (g_rows, n_seq), 1) < n_seq // 2
-    gate_ref[0] = jnp.where(low, gates[:g_rows, :], turned[g_rows:, :])
-    gate_ref[1] = jnp.where(low, turned[:g_rows, :], gates[g_rows:, :])
+    gates = e / jnp.sum(e, axis=0, keepdims=True)
+    picked = jnp.concatenate([jnp.sum(jnp.where(e_iota == ids[i:i + 1, :], gates, 0.0), axis=0, keepdims=True) for i in range(ids.shape[0])], axis=0)
+    ids32 = ids.astype(F32)
+    low = lax.broadcasted_iota(jnp.int32, ids.shape, 1) < n_seq // 2
+    gate_ref[0] = jnp.where(low, picked, pltpu.roll(ids32, n_seq // 2, 1))
+    gate_ref[1] = jnp.where(low, pltpu.roll(picked, n_seq // 2, 1), ids32)
 
     for copy in k_out + v_out:
         copy.wait()
@@ -174,7 +185,6 @@
     t_max, n_kv, hd, _ = k_t.shape
     hq, hk = w_q.shape[1], w_k.shape[1]
     n_heads = hq // hd
-    n_exp = w_router_t.shape[0]
     vm = pl.BlockSpec(memory_space=pltpu.VMEM)
     hbm = pl.BlockSpec(memory_space=pltpu.HBM)
     small = (hidden, lens, ids_t, ln_attn, q_gain, k_gain, ln_moe, w_router_t)
@@ -185,7 +195,7 @@
             jax.ShapeDtypeStruct(v_t.shape, v_t.dtype),
             jax.ShapeDtypeStruct((n_seq, d), F32),
             jax.ShapeDtypeStruct((n_seq, d), BF16),
-            jax.ShapeDtypeStruct((2, n_exp // 2, n_seq), F32),
+            jax.ShapeDtypeStruct((2, ids_t.shape[0], n_seq), F32),
         ),
         in_specs=[hbm] * 14,
         out_specs=(hbm, hbm, vm, vm, vm),
@@ -202,9 +212,9 @@
 
 
 def rs_order(half):
-    seq = [(half - 2, 3), (half - 1, 2), (half + 1, 0), (half, 1)]
+    seq = [(half - 2, 3), (half + 1, 0), (half - 1, 2), (half, 1)]
     last = dict((c, q) for q, c in seq)
-    for c in (3, 2, 0, 1, 2, 0, 1, 0, 1, 0):
+    for c in (0, 3, 1, 0, 2, 1, 0, 2, 1, 0):
         last[c] -= 1
         seq.append((last[c], c))
     return seq
@@ -222,7 +232,6 @@
     half = n // 2
     rows, d = r_ref.shape
     n_local = wg_hbm.shape[0]
-    g_rows = gate_ref.shape[1]
     hr = rows // 2
     qr = hr // 2
     ring = [{"ep": 2 * lax.rem(chip + 1, n) + core}, {"ep": 2 * lax.rem(chip + n - 1, n) + core}]
@@ -305,18 +314,17 @@
         cbuf[k, side, core, at, :] = total
         rs_copy(direction, u).start()
 
-    e_first = n_local * me
-    e_side = e_first // g_rows
-    e_row = e_first - e_side * g_rows
-    low_lanes = lax.broadcasted_iota(jnp.int32, (1, rows), 1) < hr
+    low_lanes = lax.broadcasted_iota(jnp.int32, gate_ref.shape[1:], 1) < hr
 
     def compute(k):
         x = xbuf[k].reshape(2 * rows, d)
         for e in range(n_local):
             for direction in range(2):
-                a, b = [gbuf[k, direction, c, pl.ds(e_row + e, 1), :] for c in range(2)]
-                ra, rb = pltpu.roll(a, hr, 1), pltpu.roll(b, hr, 1)
-                row = jnp.where(low_lanes, jnp.where(e_side == 0, a, ra), jnp.where(e_side == 0, rb, b))
+                a, b = gbuf[k, direction, 0], gbuf[k, direction, 1]
+                mine = (n_local * me + e).astype(F32)
+                both = jnp.where(low_lanes, a, pltpu.roll(b, hr, 1))
+                ids = jnp.where(low_lanes, pltpu.roll(a, hr, 1), b)
+                row = jnp.max(jnp.where(ids == mine, both, -1.0), axis=0, keepdims=True)
                 gcol[e, direction * rows:(direction + 1) * rows, :] = jnp.transpose(jnp.broadcast_to(row, (rows, rows)))
         ft = 256
         for e in range(n_local):

time: 85.5 us -> 84.4 us (0.987)
  Pallas kernels: 84.1 us -> 82.9 us
where the time goes in v6:
time: 84.4 us; the launch traced here: 84.3 us
  Pallas kernels  82.9 us (98%)
    pallas_call x1, Pallas kernels, moe(): pl.pallas_call(functools.partial(moe_kernel, n), out_shape=jax.ShapeDtype...  73.8 us
    pallas_call x1, Pallas kernels, attend(): pl.pallas_call(attend_kernel, out_shape=(jax.ShapeDtypeStruct(k_t.shape,...  9.13 us

profile of v6, /device:TPU:21, one launch (start us, length us, event | category | flops | bytes accessed | tf_op | source)
XLA Modules:
  0.0 84.3 jit_solution(6300979201923514850)
XLA Ops:
  0.6 9.1 %attend.1 = (bf16[32,8,64,128]{3,2,1,0:T(8,128)(2,1)}, bf16[32,8,64,128]{3,2,1,0:T(8,128)(2,1)}, f32[128,1024]{1,0:T(8,128)S(1)}, bf16[128,1024]{1,0:T(8,128)(2,1)S(1)}, f32[2,8,128]{2,1,0:T(8,128)S(1)}) custom-call(bf16[128,1024]{1,0:T(8,128)(2,1)} %h_hbm.1, s32[1,128]{1,0:T(1,128)} %bitcast.17, s32[8,128]{1,0:T(8,128)} %bitcast.14, ...), custom_call_target="tpu_custom_call" | custom-call | tf_op jit(solution)/shard_map/attend/pallas_call | solution.py:191
  9.8 73.8 %moe.1 = bf16[128,1024]{1,0:T(8,128)(2,1)S(1)} custom-call(bf16[128,1024]{1,0:T(8,128)(2,1)S(1)} %get-tuple-element.8.r_ref, f32[2,8,128]{2,1,0:T(8,128)S(1)} %get-tuple-element.9.gate_ref, f32[128,1024]{1,0:T(8,128)S(1)} %get-tuple-element.10.y_ref, bf16[2,1024,512]{2,1,0:T(8,128)(2,1)} %wg_hbm.1, bf16[2,1024,512]{2,1,0:T(8,128)(2,1)} %wu_hbm.1, ...), custom_call_target="tpu_custom_call" | custom-call | tf_op jit(solution)/shard_map/moe/pallas_call | solution.py:447
  83.6 0.7 copy.21

commit v7 on v6

--- a/solution.py
+++ b/solution.py
@@ -123,6 +123,16 @@
     for i in range(0, n_kv, 2):
         vnew[i * hd:(i + 2) * hd, :] = jnp.transpose(v_proj[:, i * hd:(i + 2) * hd]).astype(BF16).astype(F32)
 
+    def v_new_body(kv, carry):
+        new = vnew[pl.ds(pl.multiple_of(kv * hd, hd), hd), :]
+        for t in range(t_max - tc, t_max):
+            vbuf[t, kv] = jnp.where(lens == t, new, vbuf[t, kv].astype(F32)).astype(BF16)
+        return carry
+
+    v_in[n_chunk - 1].wait()
+    lax.fori_loop(0, n_kv, v_new_body, 0)
+    v_out[n_chunk - 1].start()
+
     visible = lax.broadcasted_iota(jnp.int32, (t_max, n_seq), 0) <= lens
 
     def soft_body(j, carry):
@@ -134,16 +144,20 @@
     lax.fori_loop(0, n_heads, soft_body, 0, unroll=2)
 
     for c in range(n_chunk):
-        v_in[c].wait()
-
-        def v_body(kv, carry, c=c):
+        last = c == n_chunk - 1
+        if not last:
+            v_in[c].wait()
+
+        def v_body(kv, carry, c=c, last=last):
             new = vnew[pl.ds(pl.multiple_of(kv * hd, hd), hd), :]
             at = [pl.ds(pl.multiple_of((kv * grp + g) * hd, hd), hd) for g in range(grp)]
             acc = [None if c == 0 else attn[at[g], :] for g in range(grp)]
             for tt in range(tc):
                 t = c * tc + tt
-                vt = jnp.where(lens == t, new, vbuf[t, kv].astype(F32))
-                vbuf[t, kv] = vt.astype(BF16)
+                vt = vbuf[t, kv].astype(F32)
+                if not last:
+                    vt = jnp.where(lens == t, new, vt)
+                    vbuf[t, kv] = vt.astype(BF16)
                 for g in range(grp):
                     term = vt * score[kv * grp + g, t:t + 1, :]
                     acc[g] = term if acc[g] is None else acc[g] + term
@@ -152,7 +166,8 @@
             return carry
 
         lax.fori_loop(0, n_kv, v_body, 0)
-        v_out[c].start()
+        if not last:
+            v_out[c].start()
 
     w_copies[3].wait()
     a_rows = jnp.concatenate([jnp.transpose(attn[i * n_seq:(i + 1) * n_seq, :]).astype(BF16) for i in range(n_heads * hd // n_seq)], axis=1)
@@ -212,9 +227,9 @@
 
 
 def rs_order(half):
-    seq = [(half - 2, 3), (half + 1, 0), (half - 1, 2), (half, 1)]
+    seq = [(half - 2, 3), (half - 1, 2), (half + 1, 0), (half - 3, 3), (half, 1)]
     last = dict((c, q) for q, c in seq)
-    for c in (0, 3, 1, 0, 2, 1, 0, 2, 1, 0):
+    for c in (0, 2, 1, 0, 2, 1, 0, 1, 0):
         last[c] -= 1
         seq.append((last[c], c))
     return seq
@@ -357,34 +372,32 @@
             for copy in pair_copies(direction, k, core, x_src, g_src):
                 copy.start()
 
-    def body(k, carry):
-        @pl.when(k <= n - 4)
+    def body(i, carry):
+        k = jnp.where(i < half, i, i + 1 - 2 * lax.rem(i, 2))
+
+        @pl.when(i <= n - 2)
         def _():
-            take(k + 1)
-
-        @pl.when(k >= n - 2)
+            take(i + 1)
+
+        @pl.when(i == 0)
         def _():
-            take(k)
-
-        @pl.when(k == n - 3)
+            for copy in w_copies:
+                copy.wait()
+
+        @pl.when(i == n - 4)
         def _():
             for side in range(2):
                 sum_copy(n - 5, side).wait_recv()
             for direction in range(2):
                 rs_step(direction, 0)
 
-        @pl.when(k == n - 2)
+        @pl.when(i == n - 2)
         def _():
             for side in range(2):
                 sum_copy(n - 3, side).wait_recv()
             for u in range(1, 3):
                 for direction in range(2):
                     rs_step(direction, u)
-
-        @pl.when(k == 0)
-        def _():
-            for copy in w_copies:
-                copy.wait()
 
         for direction in range(2):
             for copy in pair_copies(direction, k, other, *held(direction, k, other)):

time: 84.4 us -> 83.5 us (0.989)
    pallas_call x1, Pallas kernels: 73.8 us -> 72 us  [moe(): pl.pallas_call(functools.partial(moe_kernel, n), out_shape=jax.ShapeDtype...]
    pallas_call x1, Pallas kernels: 9.13 us -> 10.1 us  [attend(): pl.pallas_call(attend_kernel, out_shape=(jax.ShapeDtypeStruct(k_t.shape,...]
where the time goes in v7:
time: 83.5 us; the launch traced here: 83.4 us
  Pallas kernels  82.1 us (98%)
    pallas_call x1, Pallas kernels, moe(): pl.pallas_call(functools.partial(moe_kernel, n), out_shape=jax.ShapeDtype...  72 us
    pallas_call x1, Pallas kernels, attend(): pl.pallas_call(attend_kernel, out_shape=(jax.ShapeDtypeStruct(k_t.shape,...  10.1 us

profile of v7, /device:TPU:21, one launch (start us, length us, event | category | flops | bytes accessed | tf_op | source)
XLA Modules:
  0.0 83.4 jit_solution(2755157134963981584)
XLA Ops:
  0.6 10.1 %attend.1 = (bf16[32,8,64,128]{3,2,1,0:T(8,128)(2,1)}, bf16[32,8,64,128]{3,2,1,0:T(8,128)(2,1)}, f32[128,1024]{1,0:T(8,128)S(1)}, bf16[128,1024]{1,0:T(8,128)(2,1)S(1)}, f32[2,8,128]{2,1,0:T(8,128)S(1)}) custom-call(bf16[128,1024]{1,0:T(8,128)(2,1)} %h_hbm.1, s32[1,128]{1,0:T(1,128)} %bitcast.17, s32[8,128]{1,0:T(8,128)} %bitcast.14, ...), custom_call_target="tpu_custom_call" | custom-call | tf_op jit(solution)/shard_map/attend/pallas_call | solution.py:206
  10.7 72.0 %moe.1 = bf16[128,1024]{1,0:T(8,128)(2,1)S(1)} custom-call(bf16[128,1024]{1,0:T(8,128)(2,1)S(1)} %get-tuple-element.8.r_ref, f32[2,8,128]{2,1,0:T(8,128)S(1)} %get-tuple-element.9.gate_ref, f32[128,1024]{1,0:T(8,128)S(1)} %get-tuple-element.10.y_ref, bf16[2,1024,512]{2,1,0:T(8,128)(2,1)} %wg_hbm.1, bf16[2,1024,512]{2,1,0:T(8,128)(2,1)} %wu_hbm.1, ...), custom_call_target="tpu_custom_call" | custom-call | tf_op jit(solution)/shard_map/moe/pallas_call | solution.py:460
  82.7 0.7 copy.21

commit v8 on v7

--- a/solution.py
+++ b/solution.py
@@ -39,11 +39,11 @@
     v_out = [pltpu.make_async_copy(vbuf.at[pl.ds(c * tc, tc)], vn_hbm.at[pl.ds(c * tc, tc)], out_sem.at[n_chunk + c]) for c in range(n_chunk)]
     small = [pltpu.make_async_copy(src, dst, small_sem.at[i]) for i, (src, dst) in enumerate((
         (h_hbm, h_ref), (lens_hbm, lens_ref), (ids_hbm, ids_ref), (ln_a_hbm, ln_a_ref), (qg_hbm, qg_ref), (kg_hbm, kg_ref), (ln_m_hbm, ln_m_ref), (wr_hbm, wr_ref)))]
-    for copy in small + w_copies[:2]:
+    for copy in small + w_copies[:2] + k_in[:1]:
         copy.start()
     for copy in small:
         copy.wait()
-    k_in[0].start()
+    k_in[1].start()
 
     def vector(ref):
         rows = ref[...].astype(F32)
@@ -80,11 +80,11 @@
             dst[i * hd + half:(i + 1) * hd, :] = (high * cos_v + low * sin_v).astype(BF16).astype(F32)
 
     w_copies[0].wait()
-    for copy in k_in[1:] + w_copies[2:3]:
+    for copy in k_in[2:]:
         copy.start()
     rope_heads(jnp.dot(x, wk[...], preferred_element_type=F32), gain_tile(kg_ref), knew, n_kv)
     w_copies[1].wait()
-    for copy in v_in + w_copies[3:]:
+    for copy in w_copies[2:3] + v_in[:1]:
         copy.start()
     rope_heads(jnp.dot(x, wq[...], preferred_element_type=F32), gain_tile(qg_ref), qrot, n_heads)
     sub = lax.broadcasted_iota(jnp.int32, (8, n_seq), 0)
@@ -100,6 +100,7 @@
 
     for c in range(n_chunk):
         k_in[c].wait()
+        (v_in[1:] + w_copies[3:])[c].start()
 
         def k_body(kv, carry, c=c):
             new = knew[pl.ds(pl.multiple_of(kv * hd, hd), hd), :]
@@ -123,16 +124,6 @@
     for i in range(0, n_kv, 2):
         vnew[i * hd:(i + 2) * hd, :] = jnp.transpose(v_proj[:, i * hd:(i + 2) * hd]).astype(BF16).astype(F32)
 
-    def v_new_body(kv, carry):
-        new = vnew[pl.ds(pl.multiple_of(kv * hd, hd), hd), :]
-        for t in range(t_max - tc, t_max):
-            vbuf[t, kv] = jnp.where(lens == t, new, vbuf[t, kv].astype(F32)).astype(BF16)
-        return carry
-
-    v_in[n_chunk - 1].wait()
-    lax.fori_loop(0, n_kv, v_new_body, 0)
-    v_out[n_chunk - 1].start()
-
     visible = lax.broadcasted_iota(jnp.int32, (t_max, n_seq), 0) <= lens
 
     def soft_body(j, carry):
@@ -144,20 +135,16 @@
     lax.fori_loop(0, n_heads, soft_body, 0, unroll=2)
 
     for c in range(n_chunk):
-        last = c == n_chunk - 1
-        if not last:
-            v_in[c].wait()
-
-        def v_body(kv, carry, c=c, last=last):
+        v_in[c].wait()
+
+        def v_body(kv, carry, c=c):
             new = vnew[pl.ds(pl.multiple_of(kv * hd, hd), hd), :]
             at = [pl.ds(pl.multiple_of((kv * grp + g) * hd, hd), hd) for g in range(grp)]
             acc = [None if c == 0 else attn[at[g], :] for g in range(grp)]
             for tt in range(tc):
                 t = c * tc + tt
-                vt = vbuf[t, kv].astype(F32)
-                if not last:
-                    vt = jnp.where(lens == t, new, vt)
-                    vbuf[t, kv] = vt.astype(BF16)
+                vt = jnp.where(lens == t, new, vbuf[t, kv].astype(F32))
+                vbuf[t, kv] = vt.astype(BF16)
                 for g in range(grp):
                     term = vt * score[kv * grp + g, t:t + 1, :]
                     acc[g] = term if acc[g] is None else acc[g] + term
@@ -166,8 +153,7 @@
             return carry
 
         lax.fori_loop(0, n_kv, v_body, 0)
-        if not last:
-            v_out[c].start()
+        v_out[c].start()
 
     w_copies[3].wait()
     a_rows = jnp.concatenate([jnp.transpose(attn[i * n_seq:(i + 1) * n_seq, :]).astype(BF16) for i in range(n_heads * hd // n_seq)], axis=1)

time: 83.5 us -> 83 us (level)
  no operation moved by 1% of the time
where the time goes in v8:
time: 83 us
  Pallas kernels  81.6 us (98%)
    pallas_call x1, Pallas kernels, moe(): pl.pallas_call(functools.partial(moe_kernel, n), out_shape=jax.ShapeDtype...  72 us
    pallas_call x1, Pallas kernels, attend(): pl.pallas_call(attend_kernel, out_shape=(jax.ShapeDtypeStruct(k_t.shape,...  9.64 us

profile of v8, /device:TPU:21, one launch (start us, length us, event | category | flops | bytes accessed | tf_op | source)
XLA Modules:
  0.0 83.0 jit_solution(9920821407991732493)
XLA Ops:
  0.6 9.6 %attend.1 = (bf16[32,8,64,128]{3,2,1,0:T(8,128)(2,1)}, bf16[32,8,64,128]{3,2,1,0:T(8,128)(2,1)}, f32[128,1024]{1,0:T(8,128)S(1)}, bf16[128,1024]{1,0:T(8,128)(2,1)S(1)}, f32[2,8,128]{2,1,0:T(8,128)S(1)}) custom-call(bf16[128,1024]{1,0:T(8,128)(2,1)} %h_hbm.1, s32[1,128]{1,0:T(1,128)} %bitcast.17, s32[8,128]{1,0:T(8,128)} %bitcast.14, ...), custom_call_target="tpu_custom_call" | custom-call | tf_op jit(solution)/shard_map/attend/pallas_call | solution.py:192
  10.3 72.0 %moe.1 = bf16[128,1024]{1,0:T(8,128)(2,1)S(1)} custom-call(bf16[128,1024]{1,0:T(8,128)(2,1)S(1)} %get-tuple-element.8.r_ref, f32[2,8,128]{2,1,0:T(8,128)S(1)} %get-tuple-element.9.gate_ref, f32[128,1024]{1,0:T(8,128)S(1)} %get-tuple-element.10.y_ref, bf16[2,1024,512]{2,1,0:T(8,128)(2,1)} %wg_hbm.1, bf16[2,1024,512]{2,1,0:T(8,128)(2,1)} %wu_hbm.1, ...), custom_call_target="tpu_custom_call" | custom-call | tf_op jit(solution)/shard_map/moe/pallas_call | solution.py:446
  82.3 0.7 copy.21

commit v9 on v8

--- a/solution.py
+++ b/solution.py
@@ -39,11 +39,12 @@
     v_out = [pltpu.make_async_copy(vbuf.at[pl.ds(c * tc, tc)], vn_hbm.at[pl.ds(c * tc, tc)], out_sem.at[n_chunk + c]) for c in range(n_chunk)]
     small = [pltpu.make_async_copy(src, dst, small_sem.at[i]) for i, (src, dst) in enumerate((
         (h_hbm, h_ref), (lens_hbm, lens_ref), (ids_hbm, ids_ref), (ln_a_hbm, ln_a_ref), (qg_hbm, qg_ref), (kg_hbm, kg_ref), (ln_m_hbm, ln_m_ref), (wr_hbm, wr_ref)))]
-    for copy in small + w_copies[:2] + k_in[:1]:
+    for copy in small + w_copies[:2]:
         copy.start()
     for copy in small:
         copy.wait()
-    k_in[1].start()
+    for copy in k_in:
+        copy.start()
 
     def vector(ref):
         rows = ref[...].astype(F32)
@@ -80,12 +81,10 @@
             dst[i * hd + half:(i + 1) * hd, :] = (high * cos_v + low * sin_v).astype(BF16).astype(F32)
 
     w_copies[0].wait()
-    for copy in k_in[2:]:
+    for copy in w_copies[2:3] + v_in + w_copies[3:]:
         copy.start()
     rope_heads(jnp.dot(x, wk[...], preferred_element_type=F32), gain_tile(kg_ref), knew, n_kv)
     w_copies[1].wait()
-    for copy in w_copies[2:3] + v_in[:1]:
-        copy.start()
     rope_heads(jnp.dot(x, wq[...], preferred_element_type=F32), gain_tile(qg_ref), qrot, n_heads)
     sub = lax.broadcasted_iota(jnp.int32, (8, n_seq), 0)
 
@@ -100,7 +99,6 @@
 
     for c in range(n_chunk):
         k_in[c].wait()
-        (v_in[1:] + w_copies[3:])[c].start()
 
         def k_body(kv, carry, c=c):
             new = knew[pl.ds(pl.multiple_of(kv * hd, hd), hd), :]
@@ -213,9 +211,9 @@
 
 
 def rs_order(half):
-    seq = [(half - 2, 3), (half - 1, 2), (half + 1, 0), (half - 3, 3), (half, 1)]
+    seq = [(half - 2, 3), (half + 1, 0), (half - 1, 2), (half, 1)]
     last = dict((c, q) for q, c in seq)
-    for c in (0, 2, 1, 0, 2, 1, 0, 1, 0):
+    for c in (0, 3, 1, 0, 2, 1, 0, 2, 1, 0):
         last[c] -= 1
         seq.append((last[c], c))
     return seq

time: 83 us -> 82.5 us (level)
  no operation moved by 1% of the time
where the time goes in v9:
time: 82.5 us
  Pallas kernels  81.1 us (98%)
    pallas_call x1, Pallas kernels, moe(): pl.pallas_call(functools.partial(moe_kernel, n), out_shape=jax.ShapeDtype...  72 us
    pallas_call x1, Pallas kernels, attend(): pl.pallas_call(attend_kernel, out_shape=(jax.ShapeDtypeStruct(k_t.shape,...  9.12 us

profile of v9, /device:TPU:21, one launch (start us, length us, event | category | flops | bytes accessed | tf_op | source)
XLA Modules:
  0.0 82.5 jit_solution(10445186405722849584)
XLA Ops:
  0.6 9.1 %attend.1 = (bf16[32,8,64,128]{3,2,1,0:T(8,128)(2,1)}, bf16[32,8,64,128]{3,2,1,0:T(8,128)(2,1)}, f32[128,1024]{1,0:T(8,128)S(1)}, bf16[128,1024]{1,0:T(8,128)(2,1)S(1)}, f32[2,8,128]{2,1,0:T(8,128)S(1)}) custom-call(bf16[128,1024]{1,0:T(8,128)(2,1)} %h_hbm.1, s32[1,128]{1,0:T(1,128)} %bitcast.17, s32[8,128]{1,0:T(8,128)} %bitcast.14, ...), custom_call_target="tpu_custom_call" | custom-call | tf_op jit(solution)/shard_map/attend/pallas_call | solution.py:190
  9.8 72.0 %moe.1 = bf16[128,1024]{1,0:T(8,128)(2,1)S(1)} custom-call(bf16[128,1024]{1,0:T(8,128)(2,1)S(1)} %get-tuple-element.8.r_ref, f32[2,8,128]{2,1,0:T(8,128)S(1)} %get-tuple-element.9.gate_ref, f32[128,1024]{1,0:T(8,128)S(1)} %get-tuple-element.10.y_ref, bf16[2,1024,512]{2,1,0:T(8,128)(2,1)} %wg_hbm.1, bf16[2,1024,512]{2,1,0:T(8,128)(2,1)} %wu_hbm.1, ...), custom_call_target="tpu_custom_call" | custom-call | tf_op jit(solution)/shard_map/moe/pallas_call | solution.py:444
  81.8 0.7 copy.21

commit v10 on v9

--- a/solution.py
+++ b/solution.py
@@ -23,7 +23,7 @@
                   wq_hbm, wk_hbm, wv_hbm, wo_hbm, kc_hbm, vc_hbm,
                   kn_hbm, vn_hbm, y_ref, r_ref, gate_ref,
                   h_ref, lens_ref, ids_ref, ln_a_ref, qg_ref, kg_ref, ln_m_ref, wr_ref,
-                  kbuf, vbuf, wq, wk, wv, wo, qrot, knew, vnew, score, attn, small_sem, in_sem, out_sem):
+                  kbuf, vbuf, wq, wk, wv, wo, qrot, knew, vnew, score, attn, small_sem, piece_sem, in_sem, out_sem):
     t_max, n_kv, hd, n_seq = kc_hbm.shape
     n_heads = wq_hbm.shape[1] // hd
     grp = n_heads // n_kv
@@ -31,15 +31,17 @@
     n_chunk = 4
     tc = t_max // n_chunk
 
-    w_copies = [pltpu.make_async_copy(src, dst, in_sem.at[i])
-                for i, (src, dst) in enumerate(((wk_hbm, wk), (wq_hbm, wq), (wv_hbm, wv), (wo_hbm, wo)))]
+    w_copies = [pltpu.make_async_copy(src, dst, in_sem.at[i]) for i, (src, dst) in enumerate(((wv_hbm, wv), (wo_hbm, wo)))]
+    piece = 8 * hd
+    k_pieces, q_pieces = [[(pltpu.make_async_copy(src.at[:, pl.ds(i * piece, piece)], dst.at[:, pl.ds(i * piece, piece)], piece_sem.at[first + i]), i)
+                           for i in range(src.shape[1] // piece)] for src, dst, first in ((wk_hbm, wk, 0), (wq_hbm, wq, n_heads // 8))]
     k_in = [pltpu.make_async_copy(kc_hbm.at[pl.ds(c * tc, tc)], kbuf.at[pl.ds(c * tc, tc)], in_sem.at[4 + c]) for c in range(n_chunk)]
     v_in = [pltpu.make_async_copy(vc_hbm.at[pl.ds(c * tc, tc)], vbuf.at[pl.ds(c * tc, tc)], in_sem.at[4 + n_chunk + c]) for c in range(n_chunk)]
     k_out = [pltpu.make_async_copy(kbuf.at[pl.ds(c * tc, tc)], kn_hbm.at[pl.ds(c * tc, tc)], out_sem.at[c]) for c in range(n_chunk)]
     v_out = [pltpu.make_async_copy(vbuf.at[pl.ds(c * tc, tc)], vn_hbm.at[pl.ds(c * tc, tc)], out_sem.at[n_chunk + c]) for c in range(n_chunk)]
     small = [pltpu.make_async_copy(src, dst, small_sem.at[i]) for i, (src, dst) in enumerate((
         (h_hbm, h_ref), (lens_hbm, lens_ref), (ids_hbm, ids_ref), (ln_a_hbm, ln_a_ref), (qg_hbm, qg_ref), (kg_hbm, kg_ref), (ln_m_hbm, ln_m_ref), (wr_hbm, wr_ref)))]
-    for copy in small + w_copies[:2]:
+    for copy in small + [c for c, _ in k_pieces + q_pieces]:
         copy.start()
     for copy in small:
         copy.wait()
@@ -69,23 +71,32 @@
         row = jnp.concatenate([row] * (n_seq // hd), axis=1)
         return jnp.transpose(jnp.broadcast_to(row, (n_seq, n_seq)))[:hd, :]
 
-    def rope_heads(proj, gain, dst, heads):
-        for i in range(heads):
-            if i % 2 == 0:
-                pair = jnp.transpose(proj[:, i * hd:(i + 2) * hd])
-            vals = pair[(i % 2) * hd:(i % 2 + 1) * hd, :]
-            ms = jnp.mean(vals * vals, axis=0, keepdims=True)
-            vals = vals * lax.rsqrt(ms + EPS) * gain
-            low, high = vals[:half, :], vals[half:, :]
-            dst[i * hd:i * hd + half, :] = (low * cos_v - high * sin_v).astype(BF16).astype(F32)
-            dst[i * hd + half:(i + 1) * hd, :] = (high * cos_v + low * sin_v).astype(BF16).astype(F32)
-
-    w_copies[0].wait()
-    for copy in w_copies[2:3] + v_in + w_copies[3:]:
-        copy.start()
-    rope_heads(jnp.dot(x, wk[...], preferred_element_type=F32), gain_tile(kg_ref), knew, n_kv)
-    w_copies[1].wait()
-    rope_heads(jnp.dot(x, wq[...], preferred_element_type=F32), gain_tile(qg_ref), qrot, n_heads)
+    def rope_heads(proj, gain, dst, first):
+        for i in range(0, proj.shape[1] // hd, 2):
+            pair = jnp.transpose(proj[:, i * hd:(i + 2) * hd])
+            for j in range(2):
+                vals = pair[j * hd:(j + 1) * hd, :]
+                ms = jnp.mean(vals * vals, axis=0, keepdims=True)
+                vals = vals * lax.rsqrt(ms + EPS) * gain
+                low, high = vals[:half, :], vals[half:, :]
+                at = first + (i + j) * hd
+                dst[at:at + half, :] = (low * cos_v - high * sin_v).astype(BF16).astype(F32)
+                dst[at + half:at + hd, :] = (high * cos_v + low * sin_v).astype(BF16).astype(F32)
+
+    k_gain, q_gain = gain_tile(kg_ref), gain_tile(qg_ref)
+    held = None
+    for pieces, w, gain, dst in ((k_pieces, wk, k_gain, knew), (q_pieces, wq, q_gain, qrot)):
+        for copy, i in pieces:
+            copy.wait()
+            if held is None:
+                for other in w_copies[:1] + v_in + w_copies[1:]:
+                    other.start()
+            proj = jnp.dot(x, w[:, i * piece:(i + 1) * piece], preferred_element_type=F32)
+            if held is not None:
+                rope_heads(*held)
+            held = proj, gain, dst, i * piece
+    rope_heads(*held)
+
     sub = lax.broadcasted_iota(jnp.int32, (8, n_seq), 0)
 
     def fold(terms):
@@ -117,7 +128,7 @@
         lax.fori_loop(0, n_kv, k_body, 0)
         k_out[c].start()
 
-    w_copies[2].wait()
+    w_copies[0].wait()
     v_proj = jnp.dot(x, wv[...], preferred_element_type=F32)
     for i in range(0, n_kv, 2):
         vnew[i * hd:(i + 2) * hd, :] = jnp.transpose(v_proj[:, i * hd:(i + 2) * hd]).astype(BF16).astype(F32)
@@ -148,12 +159,16 @@
                     acc[g] = term if acc[g] is None else acc[g] + term
             for g in range(grp):
                 attn[at[g], :] = acc[g]
+            if c == n_chunk - 1:
+                head = pl.ds(c * tc, tc), pl.ds(kv, 1)
+                pltpu.make_async_copy(vbuf.at[head], vn_hbm.at[head], out_sem.at[n_chunk + c]).start()
             return carry
 
         lax.fori_loop(0, n_kv, v_body, 0)
-        v_out[c].start()
-
-    w_copies[3].wait()
+        if c < n_chunk - 1:
+            v_out[c].start()
+
+    w_copies[1].wait()
     a_rows = jnp.concatenate([jnp.transpose(attn[i * n_seq:(i + 1) * n_seq, :]).astype(BF16) for i in range(n_heads * hd // n_seq)], axis=1)
     y = h32 + jnp.dot(a_rows, wo[...], preferred_element_type=F32)
     y_ref[...] = y
@@ -203,7 +218,7 @@
             pltpu.VMEM(w_q.shape, BF16), pltpu.VMEM(w_k.shape, BF16), pltpu.VMEM(w_v.shape, BF16), pltpu.VMEM(w_o.shape, BF16),
             pltpu.VMEM((hq, n_seq), F32), pltpu.VMEM((hk, n_seq), F32), pltpu.VMEM((hk, n_seq), F32),
             pltpu.VMEM((n_heads, t_max, n_seq), F32), pltpu.VMEM((hq, n_seq), F32),
-            pltpu.SemaphoreType.DMA((len(small),)), pltpu.SemaphoreType.DMA((12,)), pltpu.SemaphoreType.DMA((8,)),
+            pltpu.SemaphoreType.DMA((len(small),)), pltpu.SemaphoreType.DMA((2 * n_heads // 8,)), pltpu.SemaphoreType.DMA((12,)), pltpu.SemaphoreType.DMA((8,)),
         ],
         compiler_params=pltpu.CompilerParams(vmem_limit_bytes=30 * 1024 * 1024),
         name="attend",

time: 82.5 us -> 82.8 us (level)
  no operation moved by 1% of the time
where the time goes in v10:
time: 82.8 us
  Pallas kernels  81.4 us (98%)
    pallas_call x1, Pallas kernels, moe(): pl.pallas_call(functools.partial(moe_kernel, n), out_shape=jax.ShapeDtype...  72 us
    pallas_call x1, Pallas kernels, attend(): pl.pallas_call(attend_kernel, out_shape=(jax.ShapeDtypeStruct(k_t.shape,...  9.43 us

profile of v10, /device:TPU:21, one launch (start us, length us, event | category | flops | bytes accessed | tf_op | source)
XLA Modules:
  0.0 82.8 jit_solution(13871910875770375078)
XLA Ops:
  0.6 9.4 %attend.1 = (bf16[32,8,64,128]{3,2,1,0:T(8,128)(2,1)}, bf16[32,8,64,128]{3,2,1,0:T(8,128)(2,1)}, f32[128,1024]{1,0:T(8,128)S(1)}, bf16[128,1024]{1,0:T(8,128)(2,1)S(1)}, f32[2,8,128]{2,1,0:T(8,128)S(1)}) custom-call(bf16[128,1024]{1,0:T(8,128)(2,1)} %h_hbm.1, s32[1,128]{1,0:T(1,128)} %bitcast.17, s32[8,128]{1,0:T(8,128)} %bitcast.14, ...), custom_call_target="tpu_custom_call" | custom-call | tf_op jit(solution)/shard_map/attend/pallas_call | solution.py:205
  10.1 72.0 %moe.1 = bf16[128,1024]{1,0:T(8,128)(2,1)S(1)} custom-call(bf16[128,1024]{1,0:T(8,128)(2,1)S(1)} %get-tuple-element.8.r_ref, f32[2,8,128]{2,1,0:T(8,128)S(1)} %get-tuple-element.9.gate_ref, f32[128,1024]{1,0:T(8,128)S(1)} %get-tuple-element.10.y_ref, bf16[2,1024,512]{2,1,0:T(8,128)(2,1)} %wg_hbm.1, bf16[2,1024,512]{2,1,0:T(8,128)(2,1)} %wu_hbm.1, ...), custom_call_target="tpu_custom_call" | custom-call | tf_op jit(solution)/shard_map/moe/pallas_call | solution.py:459
  82.0 0.7 copy.21

commit v11 on v9

--- a/solution.py
+++ b/solution.py
@@ -21,7 +21,7 @@
 
 def attend_kernel(h_hbm, lens_hbm, ids_hbm, ln_a_hbm, qg_hbm, kg_hbm, ln_m_hbm, wr_hbm,
                   wq_hbm, wk_hbm, wv_hbm, wo_hbm, kc_hbm, vc_hbm,
-                  kn_hbm, vn_hbm, y_ref, r_ref, gate_ref,
+                  kn_hbm, vn_hbm, y_ref, r_ref, gate_ref, v_last,
                   h_ref, lens_ref, ids_ref, ln_a_ref, qg_ref, kg_ref, ln_m_ref, wr_ref,
                   kbuf, vbuf, wq, wk, wv, wo, qrot, knew, vnew, score, attn, small_sem, in_sem, out_sem):
     t_max, n_kv, hd, n_seq = kc_hbm.shape
@@ -36,7 +36,7 @@
     k_in = [pltpu.make_async_copy(kc_hbm.at[pl.ds(c * tc, tc)], kbuf.at[pl.ds(c * tc, tc)], in_sem.at[4 + c]) for c in range(n_chunk)]
     v_in = [pltpu.make_async_copy(vc_hbm.at[pl.ds(c * tc, tc)], vbuf.at[pl.ds(c * tc, tc)], in_sem.at[4 + n_chunk + c]) for c in range(n_chunk)]
     k_out = [pltpu.make_async_copy(kbuf.at[pl.ds(c * tc, tc)], kn_hbm.at[pl.ds(c * tc, tc)], out_sem.at[c]) for c in range(n_chunk)]
-    v_out = [pltpu.make_async_copy(vbuf.at[pl.ds(c * tc, tc)], vn_hbm.at[pl.ds(c * tc, tc)], out_sem.at[n_chunk + c]) for c in range(n_chunk)]
+    v_out = [pltpu.make_async_copy(vbuf.at[pl.ds(c * tc, tc)], vn_hbm.at[pl.ds(c * tc, tc)], out_sem.at[n_chunk + c]) for c in range(n_chunk - 1)]
     small = [pltpu.make_async_copy(src, dst, small_sem.at[i]) for i, (src, dst) in enumerate((
         (h_hbm, h_ref), (lens_hbm, lens_ref), (ids_hbm, ids_ref), (ln_a_hbm, ln_a_ref), (qg_hbm, qg_ref), (kg_hbm, kg_ref), (ln_m_hbm, ln_m_ref), (wr_hbm, wr_ref)))]
     for copy in small + w_copies[:2]:
@@ -142,7 +142,10 @@
             for tt in range(tc):
                 t = c * tc + tt
                 vt = jnp.where(lens == t, new, vbuf[t, kv].astype(F32))
-                vbuf[t, kv] = vt.astype(BF16)
+                if c < n_chunk - 1:
+                    vbuf[t, kv] = vt.astype(BF16)
+                else:
+                    v_last[tt, kv] = vt.astype(BF16)
                 for g in range(grp):
                     term = vt * score[kv * grp + g, t:t + 1, :]
                     acc[g] = term if acc[g] is None else acc[g] + term
@@ -151,7 +154,8 @@
             return carry
 
         lax.fori_loop(0, n_kv, v_body, 0)
-        v_out[c].start()
+        if c < n_chunk - 1:
+            v_out[c].start()
 
     w_copies[3].wait()
     a_rows = jnp.concatenate([jnp.transpose(attn[i * n_seq:(i + 1) * n_seq, :]).astype(BF16) for i in range(n_heads * hd // n_seq)], axis=1)
@@ -195,9 +199,10 @@
             jax.ShapeDtypeStruct((n_seq, d), F32),
             jax.ShapeDtypeStruct((n_seq, d), BF16),
             jax.ShapeDtypeStruct((2, ids_t.shape[0], n_seq), F32),
+            pltpu.VMEM((t_max // 4,) + v_t.shape[1:], v_t.dtype),
         ),
         in_specs=[hbm] * 14,
-        out_specs=(hbm, hbm, vm, vm, vm),
+        out_specs=(hbm, hbm, vm, vm, vm, vm),
         scratch_shapes=[pltpu.VMEM(a.shape, a.dtype) for a in small] + [
             pltpu.VMEM(k_t.shape, BF16), pltpu.VMEM(v_t.shape, BF16),
             pltpu.VMEM(w_q.shape, BF16), pltpu.VMEM(w_k.shape, BF16), pltpu.VMEM(w_v.shape, BF16), pltpu.VMEM(w_o.shape, BF16),
@@ -466,6 +471,31 @@
     )(r, gates, y, *in_hbm(w_gate, w_up, w_down))
 
 
+def finish_kernel(out_ref, v_last, v_in_hbm, out_hbm, v_hbm, sem):
+    rows = v_last.shape[0]
+    copies = [pltpu.make_async_copy(v_last, v_hbm.at[pl.ds(v_hbm.shape[0] - rows, rows)], sem.at[0]),
+              pltpu.make_async_copy(out_ref, out_hbm, sem.at[1])]
+    for copy in copies:
+        copy.start()
+    for copy in copies:
+        copy.wait()
+
+
+def finish(out, v_last, v_new):
+    vm = pl.BlockSpec(memory_space=pltpu.VMEM)
+    hbm = pl.BlockSpec(memory_space=pltpu.HBM)
+    return pl.pallas_call(
+        finish_kernel,
+        out_shape=(jax.ShapeDtypeStruct(out.shape, out.dtype), jax.ShapeDtypeStruct(v_new.shape, v_new.dtype)),
+        in_specs=[vm, vm, hbm],
+        out_specs=(hbm, hbm),
+        scratch_shapes=[pltpu.SemaphoreType.DMA((2,))],
+        input_output_aliases={2: 1},
+        compiler_params=pltpu.CompilerParams(vmem_limit_bytes=4 * 1024 * 1024),
+        name="finish",
+    )(out, pltpu.with_memory_space_constraint(v_last, pltpu.VMEM), v_new)
+
+
 def solution(mesh):
     n_ep = mesh.shape['ep']
     row_spec = P(('dp', 'ep'), None)
@@ -478,10 +508,10 @@
     def local_step(hidden, k_cache, v_cache, seq_lens, expert_ids, ln_attn, w_q, w_k, w_v, q_gain, k_gain, w_o, ln_moe, w_router, w_gate, w_up, w_down):
         k_t = jnp.transpose(k_cache, (1, 2, 3, 0))
         v_t = jnp.transpose(v_cache, (1, 2, 3, 0))
-        k_new, v_new, y, r, gates = attend(
+        k_new, v_new, y, r, gates, v_last = attend(
             hidden, k_t, v_t, seq_lens[None, :], expert_ids.T, ln_attn.reshape(-1, 128), w_q, w_k, w_v,
             q_gain[None, :], k_gain[None, :], w_o, ln_moe.reshape(-1, 128), w_router.T)
-        out = moe(n_ep, r, gates, y, w_gate, w_up, w_down)
+        out, v_new = finish(moe(n_ep, r, gates, y, w_gate, w_up, w_down), v_last, v_new)
         return out, jnp.transpose(k_new, (3, 0, 1, 2)), jnp.transpose(v_new, (3, 0, 1, 2))
 
     return jax.shard_map(local_step, mesh=mesh, in_specs=(row_spec, cache_spec, cache_spec, len_spec, row_spec, rep_vec, rep_mat, rep_mat, rep_mat, rep_vec, rep_vec, rep_mat, rep_vec, rep_mat, exp_spec, exp_spec, exp_spec), out_specs=(row_spec, cache_spec, cache_spec), check_vma=False)

time: 82.5 us -> 82.9 us (level)
  Pallas kernels: 81.1 us -> 82.1 us
    pallas_call x0 -> x1, Pallas kernels: none -> 1.07 us  [finish(): pl.pallas_call(finish_kernel, out_shape=(jax.ShapeDtypeStruct(out.shape,...]
where the time goes in v11:
time: 82.9 us; the launch traced here: 82.8 us
  Pallas kernels  82.1 us (99%)
    pallas_call x1, Pallas kernels, moe(): pl.pallas_call(functools.partial(moe_kernel, n), out_shape=jax.ShapeDtype...  72 us
    pallas_call x1, Pallas kernels, attend(): pl.pallas_call(attend_kernel, out_shape=(jax.ShapeDtypeStruct(k_t.shape,...  9.09 us

profile of v11, /device:TPU:21, one launch (start us, length us, event | category | flops | bytes accessed | tf_op | source)
XLA Modules:
  0.0 82.8 jit_solution(3971366300708134758)
XLA Ops:
  0.6 9.1 %attend.1 = (bf16[32,8,64,128]{3,2,1,0:T(8,128)(2,1)}, bf16[32,8,64,128]{3,2,1,0:T(8,128)(2,1)}, f32[128,1024]{1,0:T(8,128)S(1)}, bf16[128,1024]{1,0:T(8,128)(2,...) custom-call(bf16[128,1024]{1,0:T(8,128)(2,1)} %h_hbm.1, s32[1,128]{1,0:T(1,128)} %bitcast.18, ...), custom_call_target="tpu_custom_call" | custom-call | tf_op jit(solution)/shard_map/attend/pallas_call | solution.py:194
  9.7 72.0 %moe.1.out_ref = bf16[128,1024]{1,0:T(8,128)(2,1)S(1)} custom-call(bf16[128,1024]{1,0:T(8,128)(2,1)S(1)} %get-tuple-element.11.r_ref, f32[2,8,128]{2,1,0:T(8,128)S(1)} %get-tuple-element.12.gate_ref, f32[128,1024]{1,0:T(8,128)S(1)} %get-tuple-element.13.y_ref, bf16[2,1024,512]{2,1,0:T(8,128)(2,1)} %wg_hbm.1, bf16[2,1024,512]{2,1,0:T(8,128)(2,1)} %wu_hbm.1, ...), custom_call_target="tpu_custom_call" | custom-call | tf_op jit(solution)/shard_map/moe/pallas_call | solution.py:449
  81.7 1.1 %finish.1 = (bf16[128,1024]{1,0:T(8,128)(2,1)}, bf16[32,8,64,128]{3,2,1,0:T(8,128)(2,1)}) custom-call(bf16[128,1024]{1,0:T(8,128)(2,1)S(1)} %moe.1.out_ref, bf16[8,8,64,128]{3,2,1,0:T(8,128)(2,1)S(1)} %get-tuple-element.14.v_last, bf16[32,8,64,128]{3,2,1,0:T(8,128)(2,1)} %get-tuple-element.15.v_in_hbm), custom_call_target="tpu_custom_call", output_to_operand_aliasing={{1}: (2, {})} | custom-call | tf_op jit(solution)/shard_map/finish/pallas_call | solution.py:487

commit v12 on v9

--- a/solution.py
+++ b/solution.py
@@ -43,8 +43,6 @@
         copy.start()
     for copy in small:
         copy.wait()
-    for copy in k_in:
-        copy.start()
 
     def vector(ref):
         rows = ref[...].astype(F32)
@@ -81,10 +79,12 @@
             dst[i * hd + half:(i + 1) * hd, :] = (high * cos_v + low * sin_v).astype(BF16).astype(F32)
 
     w_copies[0].wait()
-    for copy in w_copies[2:3] + v_in + w_copies[3:]:
+    for copy in k_in[:2]:
         copy.start()
     rope_heads(jnp.dot(x, wk[...], preferred_element_type=F32), gain_tile(kg_ref), knew, n_kv)
     w_copies[1].wait()
+    for copy in k_in[2:] + w_copies[2:3]:
+        copy.start()
     rope_heads(jnp.dot(x, wq[...], preferred_element_type=F32), gain_tile(qg_ref), qrot, n_heads)
     sub = lax.broadcasted_iota(jnp.int32, (8, n_seq), 0)
 
@@ -99,6 +99,8 @@
 
     for c in range(n_chunk):
         k_in[c].wait()
+        for copy in (v_in[:2], v_in[2:], w_copies[3:], [])[c]:
+            copy.start()
 
         def k_body(kv, carry, c=c):
             new = knew[pl.ds(pl.multiple_of(kv * hd, hd), hd), :]

time: 82.5 us -> 82.7 us (level)
  no operation moved by 1% of the time
where the time goes in v12:
time: 82.7 us
  Pallas kernels  81.3 us (98%)
    pallas_call x1, Pallas kernels, moe(): pl.pallas_call(functools.partial(moe_kernel, n), out_shape=jax.ShapeDtype...  72 us
    pallas_call x1, Pallas kernels, attend(): pl.pallas_call(attend_kernel, out_shape=(jax.ShapeDtypeStruct(k_t.shape,...  9.31 us

profile of v12, /device:TPU:21, one launch (start us, length us, event | category | flops | bytes accessed | tf_op | source)
XLA Modules:
  0.0 82.7 jit_solution(17278858916027745850)
XLA Ops:
  0.6 9.3 %attend.1 = (bf16[32,8,64,128]{3,2,1,0:T(8,128)(2,1)}, bf16[32,8,64,128]{3,2,1,0:T(8,128)(2,1)}, f32[128,1024]{1,0:T(8,128)S(1)}, bf16[128,1024]{1,0:T(8,128)(2,1)S(1)}, f32[2,8,128]{2,1,0:T(8,128)S(1)}) custom-call(bf16[128,1024]{1,0:T(8,128)(2,1)} %h_hbm.1, s32[1,128]{1,0:T(1,128)} %bitcast.17, s32[8,128]{1,0:T(8,128)} %bitcast.14, ...), custom_call_target="tpu_custom_call" | custom-call | tf_op jit(solution)/shard_map/attend/pallas_call | solution.py:192
  10.0 72.0 %moe.1 = bf16[128,1024]{1,0:T(8,128)(2,1)S(1)} custom-call(bf16[128,1024]{1,0:T(8,128)(2,1)S(1)} %get-tuple-element.8.r_ref, f32[2,8,128]{2,1,0:T(8,128)S(1)} %get-tuple-element.9.gate_ref, f32[128,1024]{1,0:T(8,128)S(1)} %get-tuple-element.10.y_ref, bf16[2,1024,512]{2,1,0:T(8,128)(2,1)} %wg_hbm.1, bf16[2,1024,512]{2,1,0:T(8,128)(2,1)} %wu_hbm.1, ...), custom_call_target="tpu_custom_call" | custom-call | tf_op jit(solution)/shard_map/moe/pallas_call | solution.py:446
  81.9 0.7 copy.21
